TPU v7x, 256 devices: a 8x8x2 block of a 8x8x16 slice. The times are simulated.
256 devices in a mesh: groups: 2 (over z), seq: 64 (over x, y), mp: 2 (over core).
Axes of the slice: x: 8, y: 8, z: 2, core: 2. Of those that a mesh axis runs over, the one named last changes fastest.
The devices are a block of a 8x8x16 slice.
Arguments:
- latent_cache: bfloat16 [16384, 64, 512], P(('groups', 'seq')), parts along dimension 0, may hold values from -6 to 6
- rope_cache: bfloat16 [16384, 4096], P(('groups', 'seq')), parts along dimension 0, may hold values from -6 to 6
- q_nope: bfloat16 [16, 128, 128], P('groups', 'mp'), parts along dimension 0, may hold values from -12 to 12
- q_rope: bfloat16 [16, 128, 64], P('groups', 'mp'), parts along dimension 0, may hold values from -2000 to 2000
- w_uk: bfloat16 [128, 128, 512], P('mp', None, 'seq'), may hold values from -0.5 to 0.5
- value_up_weight: bfloat16 [128, 512, 128], P('mp', 'seq'), may hold values from -0.25 to 0.25
- w_out: bfloat16 [16384, 7168], P('mp', 'seq'), may hold values from -0.046875 to 0.046875
- page_table: int32 [16, 2048], P('groups'), parts along dimension 0, may hold values from 0 to 8191, as said below
- lengths: int32 [16], P('groups'), parts along dimension 0, may hold values from 16384 to 131072, as said below
Outputs:
- output: bfloat16 [16, 7168], P('groups', ('seq', 'mp')), parts along dimension 0
There are 2 independent parts, one for each index of `groups`. A program takes and returns all parts, laid end to end along the dimension named above; an argument that names none is the same for every part. Nothing has to cross between parts.
Inputs may be any that keep to these rules, and one draw needn't show every extreme that they name: `lengths`: every sequence has one eighth of 131072 tokens or more; the longest has exactly 131072. page_table[b,p] for p < ceil(lengths[b] / 64) is the global slot (shard index times 128 plus local slot) holding that page; these live entries are all distinct; the other entries are 0 and unused.
All inputs are finite; a program needn't handle non-finite values.
Results may differ from a plain program's by a relative error of at most 0.012.
Values may be sent and summed in bfloat16 or wider, within the bound.
No kernel may reach another device: no remote copies, remote signals or barrier semaphores. Data moves between devices by JAX's collectives and lax.ppermute only.
A program may use at most 64 MiB of HBM per device.

v0:
```python
import jax
import jax.numpy as jnp
from jax import lax
from jax.sharding import Mesh
from jax.sharding import PartitionSpec as P

SEQ = ("seq_0", "seq_1")
GROUPS_SEQ = ("groups", "seq_0", "seq_1")
SEQ_MP = ("seq_0", "seq_1", "mp")


NEG = -1e30


def laid_out(tiles, dim):
    tiles = jnp.moveaxis(tiles, 0, dim)
    lengths = tiles.shape
    return tiles.reshape(*lengths[:dim], lengths[dim] * lengths[dim + 1], *lengths[dim + 2 :])


def from_everyone(x, axis):
    size = lax.axis_size(axis)
    return lax.all_to_all(jnp.broadcast_to(x[None], (size, *x.shape)), axis, 0, 0, tiled=True)


def collect(x, axis, dim):
    return laid_out(from_everyone(x, axis), dim)


def side_by_side(arrays, axis, split_dim, concat_dim, along):
    ends, at = ([], 0)
    for a in arrays[:-1]:
        at += a.shape[along]
        ends.append(at)
    both = jnp.concatenate(arrays, axis=along)
    return tuple(
        jnp.split(
            lax.all_to_all(both, axis, split_axis=split_dim, concat_axis=concat_dim, tiled=True),
            ends,
            axis=along,
        )
    )


def by_axis(x, axes):
    for axis in axes:
        x = lax.psum(x, axis)
    return x


def cut_along(x, dim, size):
    lengths = x.shape
    tiles = x.reshape(*lengths[:dim], size, lengths[dim] // size, *lengths[dim + 1 :])
    return jnp.moveaxis(tiles, dim, 0)


def sum_at_owner(x, axis, dim):
    size = lax.axis_size(axis)
    tiles = lax.all_to_all(cut_along(x, dim, size), axis, 0, 0, tiled=True)
    return jnp.sum(tiles, axis=0)


def local(
    latent_cache, rope_cache, q_nope, q_rope, w_uk, value_up_weight, w_out, page_table, lengths
):
    slots_dev, page_len, latent_width = latent_cache.shape
    rope_width = q_rope.shape[2]
    seq_count, heads = (q_nope.shape[0], q_nope.shape[1])
    score_scale = (q_nope.shape[2] + rope_width) ** (-0.5)
    q_part = jnp.einsum("bhn,hnk->bhk", q_nope, w_uk, preferred_element_type=jnp.float32).astype(
        jnp.bfloat16
    )
    q_latent = collect(q_part, SEQ, 2)
    first_slot = lax.axis_index(SEQ) * slots_dev
    page_count = (lengths + page_len - 1) // page_len
    logical = jnp.arange(page_table.shape[1], dtype=jnp.int32)
    live_page = logical[None, :] < page_count[:, None]
    tokens_in = jnp.clip(lengths[:, None] - page_len * logical[None, :], 0, page_len)
    local_ids = jnp.arange(slots_dev, dtype=jnp.int32)
    hits = ((page_table - first_slot)[:, :, None] == local_ids[None, None, :]) & live_page[
        :, :, None
    ]
    owner_mask = jnp.any(hits, axis=1)
    slot_fill = jnp.sum(jnp.where(hits, tokens_in[:, :, None], 0), axis=(0, 1))
    owner_half = owner_mask.astype(jnp.bfloat16)

    def update(run_state, index):
        run_max, run_sum, run_out = run_state
        start = index * 8
        latent_block = lax.dynamic_slice_in_dim(latent_cache, start, 8, 0)
        rope_block = lax.dynamic_slice_in_dim(rope_cache, start, 8, 0).reshape(
            8, page_len, rope_width
        )
        owner_block = lax.dynamic_slice_in_dim(owner_half, start, 8, 1)
        fill_block = lax.dynamic_slice_in_dim(slot_fill, start, 8, 0)
        pick_latent = jnp.einsum(
            "bs,bhk->shk", owner_block, q_latent, preferred_element_type=jnp.float32
        ).astype(jnp.bfloat16)
        pick_rope = jnp.einsum(
            "bs,bhr->shr", owner_block, q_rope, preferred_element_type=jnp.float32
        ).astype(jnp.bfloat16)
        scores = (
            jnp.einsum(
                "shk,stk->sht", pick_latent, latent_block, preferred_element_type=jnp.float32
            )
            + jnp.einsum("shr,str->sht", pick_rope, rope_block, preferred_element_type=jnp.float32)
        ) * score_scale
        live_token = (
            jnp.arange(page_len, dtype=jnp.int32)[None, None, :] < fill_block[:, None, None]
        )
        slot_max = jnp.max(jnp.where(live_token, scores, NEG), axis=2)
        exponent = jnp.where(live_token, jnp.exp(scores - slot_max[:, :, None]), 0.0)
        slot_sum = jnp.sum(exponent, axis=2)
        slot_out = jnp.einsum(
            "sht,stk->shk",
            exponent.astype(jnp.bfloat16),
            latent_block,
            preferred_element_type=jnp.float32,
        )
        owned = owner_block > 0
        candidate = jnp.where(owned[:, :, None], slot_max[None, :, :], NEG)
        new_max = jnp.maximum(run_max, jnp.max(candidate, axis=1))
        carry_scale = jnp.exp(run_max - new_max)
        factor = jnp.where(owned[:, :, None], jnp.exp(candidate - new_max[:, None, :]), 0.0)
        run_sum = run_sum * carry_scale + jnp.einsum("bsh,sh->bh", factor, slot_sum)
        run_out = run_out * carry_scale[:, :, None] + jnp.einsum("bsh,shk->bhk", factor, slot_out)
        return (new_max, run_sum, run_out)

    def visit(index, run_state):
        return update(run_state, index)

    initial = (
        jnp.full((seq_count, heads), NEG, jnp.float32),
        jnp.zeros((seq_count, heads), jnp.float32),
        jnp.zeros((seq_count, heads, latent_width), jnp.float32),
    )
    run_max, run_sum, run_out = lax.fori_loop(0, slots_dev // 8, visit, initial)
    share_width = value_up_weight.shape[1]
    shards = lax.axis_size(SEQ)
    spread_max = jnp.broadcast_to(run_max[:, :, None], (seq_count, heads, shards))
    spread_sum = jnp.broadcast_to(run_sum[:, :, None], (seq_count, heads, shards))
    peers_max, peers_sum, peers_out = (
        *side_by_side((spread_max, spread_sum), SEQ, 2, 2, 0),
        lax.all_to_all(run_out, SEQ, split_axis=2, concat_axis=2, tiled=True),
    )
    top = jnp.max(peers_max, axis=2)
    rescale = jnp.exp(peers_max - top[:, :, None])
    totals = jnp.sum(peers_sum * rescale, axis=2)
    grouped = peers_out.reshape(seq_count, heads, shards, share_width)
    shared_latent = jnp.sum(grouped * rescale[:, :, :, None], axis=2)
    local_portion = (shared_latent / totals[:, :, None]).astype(jnp.bfloat16)
    value_slice = jnp.einsum(
        "gre,req->grq", local_portion, value_up_weight, preferred_element_type=jnp.float32
    )
    value_rows = by_axis(value_slice, SEQ).astype(jnp.bfloat16)
    flat_values = value_rows.reshape(seq_count, heads * value_rows.shape[2])
    partial_out = jnp.dot(flat_values, w_out, preferred_element_type=jnp.float32)
    return sum_at_owner(partial_out, "mp", 1).astype(jnp.bfloat16)


def solution(mesh):
    finer = Mesh(
        mesh.devices.reshape(mesh.shape["groups"], 8, 8, mesh.shape["mp"]),
        ("groups", "seq_0", "seq_1", "mp"),
    )
    return jax.shard_map(
        local,
        mesh=finer,
        in_specs=(
            P(GROUPS_SEQ, None, None),
            P(GROUPS_SEQ, None),
            P("groups", "mp", None),
            P("groups", "mp", None),
            P("mp", None, SEQ),
            P("mp", SEQ, None),
            P("mp", SEQ),
            P("groups", None),
            P("groups"),
        ),
        out_specs=P("groups", SEQ_MP),
        check_vma=False,
    )
```

profile of v0, /device:TPU:513, one launch (start us, length us, event | category | flops | bytes accessed | tf_op | source)
XLA Modules:
  0.0 388.7 jit_solution(2890915873763073449)
XLA Ops:
  8.3 1.6 reshape.114
  9.8 21.8 %all-to-all-start = ((bf16[64,2,2048]{2,1,0:T(2,128)(2,1)}), bf16[64,2,2048]{2,1,0:T(2,128)(2,1)}, u32[]{:S(2)}, u32[]{:S(2)}) async-start(bf16[64,2,2048]{2,1,0:T(2,128)(2,1)} %reshape.114), calls=%async_computation | async-start | bytes 1048576 | tf_op jit(solution)/shard_map/all_to_all | solution.py:23
  31.9 5.7 %fusion.41 = pred[8,128]{1,0:T(8,128)(4,1)S(1)} fusion(s32[8,2048]{1,0:T(8,128)S(1)} %get-tuple-element.269, pred[8,2048]{1,0:T(8,128)(4,1)S(1)} %iota_compare_fusion.2), kind=kLoop, calls=%fused_computation.56 | loop fusion | flops 6290432 | bytes 82944 | tf_op jit(solution)/shard_map/reduce_or | solution.py:83
  37.7 7.8 %select_reduce_fusion.2 = s32[128]{0:T(128)S(1)} fusion(s32[8,2048]{1,0:T(8,128)S(1)} %get-tuple-element.268, s32[8,2048]{1,0:T(8,128)S(1)} %get-tuple-element.269, pred[8,2048]{1,0:T(8,128)(4,1)S(1)} %iota_compare_fusion.2), kind=kLoop, calls=%fused_computation.53 | loop fusion | flops 8388480 | bytes 147968 | tf_op jit(solution)/shard_map/reduce_sum | solution.py:84
  45.5 2.3 reshape.115
  49.1 1.9 copy.48
  51.0 138.7 %while.18 = (s32[]{:T(128)}, f32[8,64]{0,1:T(8,128)S(1)}, f32[8,64]{0,1:T(8,128)S(1)}, f32[8,64,512]{2,0,1:T(8,128)}, bf16[8,128]{1,0:T(8,128)(2,1)S(1)}, /*inde...) while((s32[]{:T(128)}, f32[8,64]{0,1:T(8,128)S(1)}, ...), condition=%wide.region_6.7_spmd.clone, body=%wide.region_2.6_spmd.clone.sunk | while | flops 81668672 | bytes 7003699 | solution.py:137
  51.4 1.4 fusion.89
  54.5 1.5 fusion.93
  57.0 1.5 fusion.94
  62.0 1.5 fusion.93
  64.5 2.7 fusion.94
  67.7 1.4 fusion.89
  70.7 1.5 fusion.93
  73.3 2.7 fusion.94
  76.4 1.4 fusion.89
  79.5 1.5 fusion.93
  82.0 2.7 fusion.94
  85.2 1.4 fusion.89
  88.2 1.5 fusion.93
  90.8 2.7 fusion.94
  93.9 1.4 fusion.89
  97.0 1.5 fusion.93
  99.5 2.7 fusion.94
  102.7 1.4 fusion.89
  105.7 1.5 fusion.93
  108.2 2.7 fusion.94
  111.4 1.4 fusion.89
  114.4 1.5 fusion.93
  117.0 2.7 fusion.94
  120.1 1.4 fusion.89
  123.2 1.5 fusion.93
  125.7 2.7 fusion.94
  128.9 1.4 fusion.89
  131.9 1.5 fusion.93
  134.5 2.7 fusion.94
  137.6 1.4 fusion.89
  140.7 1.5 fusion.93
  143.2 2.7 fusion.94
  146.4 1.4 fusion.89
  149.4 1.5 fusion.93
  151.9 2.7 fusion.94
  158.1 1.5 fusion.93
  160.7 2.7 fusion.94
  163.9 1.4 fusion.89
  166.9 1.5 fusion.93
  169.4 2.7 fusion.94
  175.6 1.5 fusion.93
  178.2 2.7 fusion.94
  181.3 1.4 fusion.89
  184.4 1.5 fusion.93
  186.9 2.7 fusion.94
  190.9 13.3 %all-to-all-start.2 = ((f32[64,1,1024]{2,1,0:T(1,128)}), f32[64,1,1024]{2,1,0:T(1,128)S(1)}, u32[]{:S(2)}, u32[]{:S(2)}) async-start(f32[64,1,1024]{2,1,0:T(1,128)} %reshape.118), calls=%async_computation.2 | async-start | bytes 524288 | tf_op jit(solution)/shard_map/all_to_all | solution.py:38
  204.3 2.3 copy.50
  206.6 3.4 reshape.116
  210.0 5.1 %all-to-all-done.2 = f32[64,1,1024]{2,1,0:T(1,128)S(1)} async-done(((f32[64,1,1024]{2,1,0:T(1,128)}), f32[64,1,1024]{2,1,0:T(1,128)S(1)}, u32[]{:S(2)}, u32[]{:S(2)}) %all-to-all-start.2) | async-done | bytes 262176 | tf_op jit(solution)/shard_map/all_to_all | solution.py:38
  215.2 7.9 %all-to-all-start.1 = ((f32[64,1,4096]{2,1,0:T(1,128)}), f32[64,1,4096]{2,1,0:T(1,128)}, u32[]{:S(2)}, u32[]{:S(2)}) async-start(f32[64,1,4096]{2,1,0:T(1,128)} %reshape.116), calls=%async_computation.1 | async-start | bytes 2097152 | tf_op jit(solution)/shard_map/all_to_all | solution.py:144
  225.3 18.9 %all-to-all-done.1 = f32[64,1,4096]{2,1,0:T(1,128)} async-done(((f32[64,1,4096]{2,1,0:T(1,128)}), f32[64,1,4096]{2,1,0:T(1,128)}, u32[]{:S(2)}, u32[]{:S(2)}) %all-to-all-start.1) | async-done | bytes 1048608 | tf_op jit(solution)/shard_map/all_to_all | solution.py:144
  244.2 4.4 %reduce = f32[64,4096]{1,0:T(8,128)S(1)} reduce(f32[64,1,4096]{2,1,0:T(1,128)} %all-to-all-done.1, f32[]{:T(128)} %broadcast.134), dimensions={1}, to_apply=%all_to_all.13.reduce_sub_computation | reduce | bytes 2097156 | tf_op jit(solution)/shard_map/all_to_all | solution.py:144
  248.6 2.2 reshape.117
  250.7 2.2 fusion.42
  254.1 82.6 %all-reduce.3.cloned.1.call-done = f32[8,64,128]{2,0,1:T(8,128)} async-done(((f32[8,64,128]{2,0,1:T(8,128)}), f32[8,64,128]{2,0,1:T(8,128)}) %all-reduce.3.cloned.1.call-update) | async-done | bytes 262160 | tf_op jit(solution)/shard_map/psum | solution.py:47
  336.7 26.8 %all-reduce.4 = bf16[8,64,128]{2,0,1:T(8,128)(2,1)S(1)} all-reduce(f32[8,64,128]{2,0,1:T(8,128)} %all-reduce.3.cloned.1.call-done), channel_id=1, replica_groups=mesh['groups'=2,'seq_0'=8,'seq_1'=8,'mp'=2] {'seq_1'}, use_global_device_ids=true, to_apply=%region_11.12 | all-reduce | flops 65536 | bytes 393216 | tf_op jit(solution)/shard_map/psum | solution.py:47
  364.5 16.0 %all_to_all.20 = f32[2,1,448]{2,1,0:T(1,128)S(1)} all-to-all(f32[2,1,448]{2,1,0:T(1,128)S(1)} %reshape.120), channel_id=1, replica_groups=mesh['groups'=2,'seq_0'=8,'seq_1'=8,'mp'=2] {'mp'}, dimensions={0} | all-to-all | bytes 7168 | tf_op jit(solution)/shard_map/all_to_all | solution.py:59
  (355 shorter events, 63.0 us)
Async XLA Ops:
  6.5 356.9 %copy-start = (bf16[8192,112]{0,1:T(8,128)(2,1)S(1)}, bf16[8192,112]{0,1:T(8,128)(2,1)}, u32[]{:S(2)}) copy-start(bf16[8192,112]{0,1:T(8,128)(2,1)} %param.17) | copy-start | bytes 5505028
  6.6 25.2 %copy-start.5 = (s32[8]{0:T(128)S(1)}, s32[8]{0:T(128)}, u32[]{:S(2)}) copy-start(s32[8]{0:T(128)} %param.19) | copy-start | bytes 100
  6.6 25.2 %copy-start.4 = (s32[8,2048]{1,0:T(8,128)S(1)}, s32[8,2048]{1,0:T(8,128)}, u32[]{:S(2)}) copy-start(s32[8,2048]{1,0:T(8,128)} %param.18) | copy-start | bytes 196612
  7.9 29.8 %copy-start.2 = (bf16[8,64,64]{2,1,0:T(8,128)(2,1)S(1)}, bf16[8,64,64]{2,1,0:T(8,128)(2,1)}, u32[]{:S(2)}) copy-start(bf16[8,64,64]{2,1,0:T(8,128)(2,1)} %param.14) | copy-start | bytes 196612
  9.8 35.7 %all-to-all-start = ((bf16[64,2,2048]{2,1,0:T(2,128)(2,1)}), bf16[64,2,2048]{2,1,0:T(2,128)(2,1)}, u32[]{:S(2)}, u32[]{:S(2)}) async-start(bf16[64,2,2048]{2,1,0:T(2,128)(2,1)} %reshape.114), calls=%async_computation | async-start | bytes 1048576 | tf_op jit(solution)/shard_map/all_to_all | solution.py:23
  189.6 14.6 %copy-start.1 = (f32[8,64,512]{2,0,1:T(8,128)S(1)}, f32[8,64,512]{2,0,1:T(8,128)}, u32[]{:S(2)}) copy-start(f32[8,64,512]{2,0,1:T(8,128)} %get-tuple-element.176) | copy-start | bytes 3145732
  190.9 24.2 %all-to-all-start.2 = ((f32[64,1,1024]{2,1,0:T(1,128)}), f32[64,1,1024]{2,1,0:T(1,128)S(1)}, u32[]{:S(2)}, u32[]{:S(2)}) async-start(f32[64,1,1024]{2,1,0:T(1,128)} %reshape.118), calls=%async_computation.2 | async-start | bytes 524288 | tf_op jit(solution)/shard_map/all_to_all | solution.py:38
  215.2 29.0 %all-to-all-start.1 = ((f32[64,1,4096]{2,1,0:T(1,128)}), f32[64,1,4096]{2,1,0:T(1,128)}, u32[]{:S(2)}, u32[]{:S(2)}) async-start(f32[64,1,4096]{2,1,0:T(1,128)} %reshape.116), calls=%async_computation.1 | async-start | bytes 2097152 | tf_op jit(solution)/shard_map/all_to_all | solution.py:144
  223.1 113.6 %all-reduce.3.cloned.1.call-start = ((), (), s32[]{:S(2)}) async-start(), calls=%async_computation.4 | async-start | bytes 524288 | tf_op jit(solution)/shard_map/psum | solution.py:47
  248.5 4.5 %copy-start.3 = (bf16[64,8,128]{2,1,0:T(8,128)(2,1)S(1)}, bf16[64,8,128]{2,1,0:T(8,128)(2,1)}, u32[]{:S(2)}) copy-start(bf16[64,8,128]{2,1,0:T(8,128)(2,1)} %param.16) | copy-start | bytes 393220
Sparse Core Ops, SparseCore 0:
  254.2 82.4 all-reduce.2
where the time goes:
time: 392 us; the launch traced here: 389 us
  matrix products  110 us (28%)
  waiting for transfers between devices  107 us (27%)
  starting transfers between devices  43.1 us (11%)
  blocking collectives  42.8 us (11%)
  local copies, waits for them, and re-layouts  42.3 us (11%)
  other arithmetic  29.5 us (8%)
  between operations  13.7 us (3%)
    psum x1, waiting for transfers between devices, by_axis(): x = lax.psum(x, axis)  82.6 us
    dot_general x16, matrix products, update(): jnp.einsum('bsh,shk->bhk', factor, slot_out)  42.6 us
    psum x1, blocking collectives, by_axis(): x = lax.psum(x, axis)  26.8 us
    dot_general x16, matrix products, update(): jnp.einsum('sht,stk->shk', exponent.astype(jnp.bfloat16), latent_block, p...  24.3 us
    dot_general x16, matrix products, update(): jnp.einsum('shk,stk->sht', pick_latent, latent_block, preferred_element_t...  22 us
    all_to_all x1, starting transfers between devices, from_everyone(): lax.all_to_all(jnp.broadcast_to(x[None], (size, *x.shape)), axis, 0, 0, t...  21.8 us
    all_to_all x1, waiting for transfers between devices, local(): lax.all_to_all(run_out, SEQ, split_axis=2, concat_axis=2, tiled=True)  18.9 us
    all_to_all x1, blocking collectives, sum_at_owner(): tiles = lax.all_to_all(cut_along(x, dim, size), axis, 0, 0, tiled=True)  16 us
  transfers between devices with their start and end apart: 4, of which 3 were waited for; matrix products, arithmetic and copies ran while one was open for 6% of the time, Pallas kernels for 0%

commit v1 on v0

v1 whole, which is shorter than its diff:
```python
import functools

import jax
import jax.numpy as jnp
from jax import lax
from jax.experimental import pallas as pl
from jax.experimental.pallas import tpu as pltpu
from jax.sharding import PartitionSpec as P

NEG = -1e30
LANES = 128
NT = (((1,), (1,)), ((), ()))


def whole(shape):
    return pl.BlockSpec(shape, lambda *_: (0,) * len(shape))


def send_query(q_ref, w_ref, v_ref, out_ref):
    seqs, heads, nope = q_ref.shape
    cols = w_ref.shape[1]
    q = q_ref[...].reshape(seqs * heads, nope)
    w = w_ref[...].reshape(heads * cols, nope)
    every = lax.dot_general(w, q, NT, preferred_element_type=jnp.float32)
    every = every.reshape(heads, cols, seqs * heads)
    head = lax.broadcasted_iota(jnp.int32, every.shape, 0)
    lane = lax.broadcasted_iota(jnp.int32, every.shape, 2)
    part = jnp.sum(jnp.where(lane % heads == head, every, 0.0), axis=0).astype(jnp.bfloat16)
    shards = out_ref.shape[0]
    tiles = seqs * heads // LANES
    for tile in range(tiles):
        piece = part[:, tile * LANES : (tile + 1) * LANES]
        out_ref[:, tile * cols : (tile + 1) * cols, :] = jnp.broadcast_to(piece[None], (shards, cols, LANES))
    out_ref[:, tiles * cols :, :] = v_ref[...]


def find_owner(page_len, first_ref, table_ref, lengths_ref, out_ref, owner_sum, fill_sum):
    seqs, pages = table_ref.shape
    slots = out_ref.shape[1]
    logical = lax.broadcasted_iota(jnp.int32, (seqs, pages), 1)
    seq = lax.broadcasted_iota(jnp.int32, (seqs, pages), 0)
    left = lengths_ref[...] - page_len * logical
    local_slot = jnp.where(left > 0, table_ref[...] - first_ref[0], -1)
    tokens = jnp.clip(left, 0, page_len)
    code = (seq * LANES + tokens).astype(jnp.float32)

    def at_slot(slot, carry):
        hit = jnp.where(local_slot == slot, code, 0.0)
        acc = hit[:, :LANES]
        for j in range(1, pages // LANES):
            acc = acc + hit[:, j * LANES : (j + 1) * LANES]
        row = jnp.sum(acc, axis=0, keepdims=True)
        owner = jnp.floor(row * (1.0 / LANES))
        owner_sum[pl.ds(slot, 1), :] = owner
        fill_sum[pl.ds(slot, 1), :] = row - owner * LANES
        return carry

    lax.fori_loop(0, slots, at_slot, 0, unroll=4)
    ones = jnp.ones((8, LANES), jnp.bfloat16)
    owner = lax.dot_general(ones, owner_sum[...].astype(jnp.bfloat16), NT, preferred_element_type=jnp.float32)
    fill = lax.dot_general(ones, fill_sum[...].astype(jnp.bfloat16), NT, preferred_element_type=jnp.float32)
    out_ref[...] = (owner * LANES + fill).astype(jnp.int32)[:1]


def attend(
    scale, chunk, code_ref, recv_ref, q_rope_ref, rope_ref, latent_hbm, out_ref,
    latent, query, scores, top, total, acc, rows, sems,
):
    slots, page_len, width = latent.shape
    seqs, heads, _ = q_rope_ref.shape
    pairs = slots // 2
    chunks = slots // chunk

    def copy_of(index):
        at = pl.ds(index * chunk, chunk)
        return pltpu.make_async_copy(latent_hbm.at[at], latent.at[at], sems.at[index])

    for index in range(chunks):
        copy_of(index).start()

    cols = recv_ref.shape[1] // (seqs * heads // LANES + 1)
    for tile in range(seqs * heads // LANES):
        block = recv_ref[:, tile * cols : (tile + 1) * cols, :].astype(jnp.float32)
        block = block.reshape(width, LANES)
        query[tile * LANES : (tile + 1) * LANES, :] = block.T.astype(jnp.bfloat16)
    top[...] = jnp.full(top.shape, NEG, jnp.float32)
    total[...] = jnp.zeros(total.shape, jnp.float32)
    acc[...] = jnp.zeros(acc.shape, jnp.float32)

    lane = lax.broadcasted_iota(jnp.int32, (heads, LANES), 1)
    left = lane < page_len

    def owners(pair):
        first, second = code_ref[0, 2 * pair], code_ref[0, 2 * pair + 1]
        return first // LANES, first % LANES, second // LANES, second % LANES

    def latent_pair(pair):
        return latent[pl.ds(2 * pair, 2)].reshape(2 * page_len, width)

    def score_pair(pair):
        a, fill_a, b, fill_b = owners(pair)
        lhs = jnp.concatenate(
            [query[pl.ds(pl.multiple_of(a * heads, heads), heads), :], query[pl.ds(pl.multiple_of(b * heads, heads), heads), :]],
            axis=0,
        )
        rot = jnp.concatenate([q_rope_ref[a], q_rope_ref[b]], axis=0)
        keys = rope_ref[pl.ds(2 * pair, 2)].reshape(2 * page_len, rope_ref.shape[2])
        both = lax.dot_general(lhs, latent_pair(pair), NT, preferred_element_type=jnp.float32)
        both = both + lax.dot_general(rot, keys, NT, preferred_element_type=jnp.float32)
        score = jnp.where(left, both[:heads], both[heads:]) * scale
        token = jnp.where(left, lane, lane - page_len)
        score = jnp.where(token < jnp.where(left, fill_a, fill_b), score, NEG)
        scores[pair] = score
        top[a] = jnp.maximum(top[a], jnp.where(left, score, NEG))
        top[b] = jnp.maximum(top[b], jnp.where(left, NEG, score))

    def score_chunk(index, carry):
        copy_of(index).wait()
        for k in range(chunk // 2):
            score_pair(index * (chunk // 2) + k)
        return carry

    lax.fori_loop(0, chunks, score_chunk, 0)

    for b in range(seqs):
        top[b] = jnp.broadcast_to(jnp.max(top[b], axis=1, keepdims=True), (heads, LANES))

    def weigh_pair(pair):
        a, _, b, _ = owners(pair)
        score = scores[pair]
        peak = jnp.where(left, top[a], top[b])
        weight = jnp.where(score > 0.5 * NEG, jnp.exp(score - peak), 0.0)
        weight_a = jnp.where(left, weight, 0.0)
        weight_b = jnp.where(left, 0.0, weight)
        total[a] = total[a] + weight_a
        total[b] = total[b] + weight_b
        lhs = jnp.concatenate([weight_a, weight_b], axis=0).astype(jnp.bfloat16)
        both = jnp.dot(lhs, latent_pair(pair), preferred_element_type=jnp.float32)
        acc[a] = acc[a] + both[:heads]
        acc[b] = acc[b] + both[heads:]

    def weigh_chunk(index, carry):
        for k in range(chunk // 2):
            weigh_pair(index * (chunk // 2) + k)
        return carry

    lax.fori_loop(0, chunks, weigh_chunk, 0)

    for piece in range(width // LANES + 1):
        for b in range(seqs):
            if piece < width // LANES:
                value = acc[b, :, piece * LANES : (piece + 1) * LANES]
            else:
                sums = jnp.broadcast_to(jnp.sum(total[b], axis=1, keepdims=True), (heads, LANES))
                value = jnp.where(lane < 3, top[b], sums)
            rows[pl.ds(b, heads, stride=seqs), :] = value
        value = rows[...]
        if piece == width // LANES:
            high = value.astype(jnp.bfloat16).astype(jnp.float32)
            middle = (value - high).astype(jnp.bfloat16).astype(jnp.float32)
            low = value - high - middle
            third = lax.broadcasted_iota(jnp.int32, value.shape, 1) % 3
            value = jnp.where(third == 0, high, jnp.where(third == 1, middle, low))
        out_ref[:, :, piece * LANES : (piece + 1) * LANES] = value.reshape(heads, seqs, LANES).astype(jnp.bfloat16)


def combine(width, peers_ref, up_ref, out_ref):
    shards, seqs, _ = peers_ref.shape
    stats = peers_ref[:, :, width:].astype(jnp.float32)
    lane = lax.broadcasted_iota(jnp.int32, stats.shape, 2)
    peak = jnp.sum(jnp.where(lane < 3, stats, 0.0), axis=2, keepdims=True)
    sums = jnp.sum(jnp.where((lane >= 3) & (lane < 6), stats, 0.0), axis=2, keepdims=True)
    rescale = jnp.exp(peak - jnp.max(peak, axis=0, keepdims=True))
    total = jnp.sum(sums * rescale, axis=0)
    mixed = jnp.sum(peers_ref[:, :, :width].astype(jnp.float32) * rescale, axis=0)
    attention = (mixed / total).astype(jnp.bfloat16)
    up = up_ref[...].astype(jnp.float32).reshape(width, up_ref.shape[2]).astype(jnp.bfloat16)
    values = jnp.dot(attention, up, preferred_element_type=jnp.float32).astype(jnp.bfloat16)
    out_ref[...] = jnp.broadcast_to(values[None], out_ref.shape)


def local(
    latent_cache, rope_cache, q_nope, q_rope, w_uk, value_up_weight, w_out, page_table, lengths
):
    slots, page_len, width = latent_cache.shape
    seqs, heads, nope = q_nope.shape
    rope = q_rope.shape[2]
    value_dim = value_up_weight.shape[2]
    cols = w_uk.shape[2]
    shards = lax.axis_size("seq")
    pages = page_table.shape[1]
    scale = (nope + rope) ** -0.5
    f32, bf16 = jnp.float32, jnp.bfloat16

    send_rows = (seqs * heads // LANES + 1) * cols
    sent = pl.pallas_call(
        send_query, out_shape=jax.ShapeDtypeStruct((shards, send_rows, LANES), bf16)
    )(q_nope, jnp.swapaxes(w_uk, 1, 2), value_up_weight)
    recv = lax.all_to_all(sent, "seq", 0, 0, tiled=True)

    first = (lax.axis_index("seq") * slots).astype(jnp.int32).reshape(1)
    code = pl.pallas_call(
        functools.partial(find_owner, page_len),
        out_shape=jax.ShapeDtypeStruct((1, slots), jnp.int32),
        in_specs=[
            pl.BlockSpec(memory_space=pltpu.SMEM),
            whole((seqs, pages)),
            whole((seqs, 1)),
        ],
        scratch_shapes=[pltpu.VMEM((slots, LANES), f32), pltpu.VMEM((slots, LANES), f32)],
    )(first, page_table, lengths.reshape(seqs, 1))
    rope_keys = rope_cache.reshape(slots, page_len, rope)

    chunk = 8
    out_width = width + LANES
    partial = pl.pallas_call(
        functools.partial(attend, scale, chunk),
        out_shape=jax.ShapeDtypeStruct((heads, seqs, out_width), bf16),
        in_specs=[
            pl.BlockSpec(memory_space=pltpu.SMEM),
            whole(recv.shape),
            whole(q_rope.shape),
            whole(rope_keys.shape),
            pl.BlockSpec(memory_space=pl.ANY),
        ],
        scratch_shapes=[
            pltpu.VMEM((slots, page_len, width), bf16),
            pltpu.VMEM((seqs * heads, width), bf16),
            pltpu.VMEM((slots // 2, heads, LANES), f32),
            pltpu.VMEM((seqs, heads, LANES), f32),
            pltpu.VMEM((seqs, heads, LANES), f32),
            pltpu.VMEM((seqs, heads, width), f32),
            pltpu.VMEM((seqs * heads, LANES), f32),
            pltpu.SemaphoreType.DMA((slots // chunk,)),
        ],
    )(code, recv, q_rope, rope_keys, latent_cache)
    peers = lax.all_to_all(partial, "seq", 0, 0, tiled=True)

    last = send_rows // cols - 1
    values = pl.pallas_call(
        functools.partial(combine, width),
        out_shape=jax.ShapeDtypeStruct((shards, seqs, value_dim), bf16),
        grid=(1,),
        in_specs=[
            whole(peers.shape),
            pl.BlockSpec((shards, cols, LANES), lambda i: (0, last, 0)),
        ],
        out_specs=whole((shards, seqs, value_dim)),
    )(peers, recv)
    every = lax.all_to_all(values, "seq", 0, 0, tiled=True)
    flat = jnp.swapaxes(every, 0, 1).reshape(seqs, heads * value_dim)
    half = jnp.dot(flat, w_out, preferred_element_type=f32)
    both = half + lax.ppermute(half, "mp", [(0, 1), (1, 0)])
    share = half.shape[1] // lax.axis_size("mp")
    return lax.dynamic_slice_in_dim(both, lax.axis_index("mp") * share, share, 1).astype(bf16)


def solution(mesh):
    return jax.shard_map(
        local,
        mesh=mesh,
        in_specs=(
            P(("groups", "seq"), None, None),
            P(("groups", "seq"), None),
            P("groups", "mp", None),
            P("groups", "mp", None),
            P("mp", None, "seq"),
            P("mp", "seq", None),
            P("mp", "seq"),
            P("groups", None),
            P("groups"),
        ),
        out_specs=P("groups", ("seq", "mp")),
        check_vma=False,
    )
```

time: 392 us -> 112 us (0.29)
  the two profiles are of different devices: /device:TPU:513 before, /device:TPU:641 now
where the time goes in v1:
time: 112 us; the launch traced here: 111 us
  blocking collectives  46.3 us (41%)
  starting transfers between devices  23.9 us (21%)
  Pallas kernels  23.2 us (21%)
  waiting for transfers between devices  9.73 us (9%)
  local copies, waits for them, and re-layouts  7.58 us (7%)
    all_to_all x1, blocking collectives, local(): peers = lax.all_to_all(partial, 'seq', 0, 0, tiled=True)  26.4 us
    all_to_all x1, starting transfers between devices, local(): recv = lax.all_to_all(sent, 'seq', 0, 0, tiled=True)  21 us
    all_to_all x1, blocking collectives, local(): every = lax.all_to_all(values, 'seq', 0, 0, tiled=True)  19.9 us
    pallas_call x1, Pallas kernels, local(): pl.pallas_call(functools.partial(attend, scale, chunk), out_shape=jax.Sha...  15.6 us
    all_to_all x1, waiting for transfers between devices, local(): recv = lax.all_to_all(sent, 'seq', 0, 0, tiled=True)  8.9 us
    reshape x1, local copies, waits for them, and re-layouts, local(): rope_keys = rope_cache.reshape(slots, page_len, rope)  3.79 us
    pallas_call x1, Pallas kernels, local(): pl.pallas_call(functools.partial(find_owner, page_len), out_shape=jax.Sha...  3.07 us
    ppermute x1, starting transfers between devices, local(): both = half + lax.ppermute(half, 'mp', [(0, 1), (1, 0)])  2.9 us
  transfers between devices with their start and end apart: 2, of which 2 were waited for; matrix products, arithmetic and copies ran while one was open for 5% of the time, Pallas kernels for 3%

profile of v1, /device:TPU:641, one launch (start us, length us, event | category | flops | bytes accessed | tf_op | source)
XLA Modules:
  0.0 111.4 jit_solution(16137595928551082937)
XLA Ops:
  0.0 0.0 copy-start
  0.0 0.0 copy-start.2
  0.0 2.4 %shard_map.92 = bf16[64,40,128]{2,1,0:T(8,128)(2,1)} custom-call(bf16[8,64,128]{2,1,0:T(8,128)(2,1)} %q_ref.1, bf16[64,8,128]{2,1,0:T(8,128)(2,1)} %bitcast.11, bf16[64,8,128]{2,1,0:T(8,128)(2,1)} %v_ref.1), custom_call_target="tpu_custom_call" | custom-call | tf_op jit(solution)/shard_map/pallas_call | solution.py:196
  2.4 21.0 %all-to-all-start = ((bf16[64,40,128]{2,1,0:T(8,128)(2,1)}), bf16[64,40,128]{2,1,0:T(8,128)(2,1)S(1)}, u32[]{:S(2)}, u32[]{:S(2)}) async-start(bf16[64,40,128]{2,1,0:T(8,128)(2,1)} %shard_map.92), calls=%async_computation | async-start | bytes 1310720 | tf_op jit(solution)/shard_map/all_to_all | solution.py:199
  23.4 0.0 copy-done.2
  23.4 0.7 copy.11.lengths_ref
  24.1 1.6 %copy.12 = bf16[128,4096]{0,1:T(8,128)(2,1)S(1)} copy(bf16[128,4096]{1,0:T(8,128)(2,1)} %param.10) | data formatting | bytes 2097152 | tf_op args[1]
  25.7 3.8 %copy.13.rope_ref = bf16[128,64,64]{2,1,0:T(8,128)(2,1)} copy(bf16[128,64,64]{0,2,1:T(8,128)(2,1)S(1)} %bitcast.10) | data formatting | bytes 2097152 | tf_op jit(solution)/shard_map/reshape | solution.py:212
  29.5 3.1 %shard_map.91.code_ref = s32[1,128]{1,0:T(1,128)} custom-call(s32[1]{0:T(128)} %bitcast.first_ref, s32[8,2048]{1,0:T(8,128)} %table_ref.1, s32[8,1]{1,0:T(8,128)} %copy.11.lengths_ref), custom_call_target="tpu_custom_call" | custom-call | tf_op jit(solution)/shard_map/pallas_call | solution.py:202
  32.5 8.9 %all-to-all-done.recv_ref.up_ref = bf16[64,40,128]{2,1,0:T(8,128)(2,1)S(1)} async-done(((bf16[64,40,128]{2,1,0:T(8,128)(2,1)}), bf16[64,40,128]{2,1,0:T(8,128)(2,1)S(1)}, u32[]{:S(2)}, u32[]{:S(2)}) %all-to-all-start) | async-done | bytes 655392 | tf_op jit(solution)/shard_map/all_to_all | solution.py:199
  41.5 0.0 copy-start.1
  41.5 0.9 copy-done.1
  42.3 15.6 %shard_map.93 = bf16[64,8,640]{2,1,0:T(8,128)(2,1)} custom-call(s32[1,128]{1,0:T(1,128)} %shard_map.91.code_ref, bf16[64,40,128]{2,1,0:T(8,128)(2,1)} %copy-done.1, bf16[8,64,64]{2,1,0:T(8,128)(2,1)} %q_rope_ref.1, bf16[128,64,64]{2,1,0:T(8,128)(2,1)} %copy.13.rope_ref, bf16[128,64,512]{2,1,0:T(8,128)(2,1)} %latent_hbm.1), custom_call_target="tpu_custom_call" | custom-call | tf_op jit(solution)/shard_map/pallas_call | solution.py:216
  57.9 26.4 %all_to_all.15.peers_ref = bf16[64,8,640]{2,1,0:T(8,128)(2,1)} all-to-all(bf16[64,8,640]{2,1,0:T(8,128)(2,1)} %shard_map.93), channel_id=1, replica_groups=mesh['groups'=2,'seq'=64,'mp'=2] {'seq'}, dimensions={0} | all-to-all | bytes 1310720 | tf_op jit(solution)/shard_map/all_to_all | solution.py:237
  84.3 2.2 %shard_map.94 = bf16[64,8,128]{2,1,0:T(8,128)(2,1)} custom-call(bf16[64,8,640]{2,1,0:T(8,128)(2,1)} %all_to_all.15.peers_ref, bf16[64,40,128]{2,1,0:T(8,128)(2,1)} %copy-done.1), custom_call_target="tpu_custom_call" | custom-call | tf_op jit(solution)/shard_map/pallas_call | solution.py:240
  86.5 19.9 %all_to_all.16 = bf16[64,8,128]{2,1,0:T(8,128)(2,1)S(1)} all-to-all(bf16[64,8,128]{2,1,0:T(8,128)(2,1)} %shard_map.94), channel_id=1, replica_groups=mesh['groups'=2,'seq'=64,'mp'=2] {'seq'}, dimensions={0} | all-to-all | bytes 262144 | tf_op jit(solution)/shard_map/all_to_all | solution.py:250
  106.4 0.0 copy-done
  106.4 0.6 fusion
  107.0 2.9 %collective-permute-start = (f32[8,112]{1,0:T(8,128)S(1)}, f32[8,112]{1,0:T(8,128)S(1)}, u32[]{:S(2)}, u32[]{:S(2)}) collective-permute-start(f32[8,112]{1,0:T(8,128)S(1)} %fusion), channel_id=1, source_target_pairs={{0,1},{1,0},{2,3},{3,2},{4,5},{5,4},{6,7},{7,6},{8,9},{9,8},{10,11... | collective-permute-start | bytes 10760 | tf_op jit(solution)/shard_map/ppermute | solution.py:253
  109.9 0.8 collective-permute-done
  110.7 0.7 dynamic-slice_convert_fusion
  (1 shorter events, 0.0 us)
Async XLA Ops:
  0.0 106.4 %copy-start = (bf16[8192,112]{0,1:T(8,128)(2,1)S(1)}, bf16[8192,112]{0,1:T(8,128)(2,1)}, u32[]{:S(2)}) copy-start(bf16[8192,112]{0,1:T(8,128)(2,1)} %param.15) | copy-start | bytes 5505028
  0.0 23.4 %copy-start.2 = (s32[8]{0:T(128)S(1)}, s32[8]{0:T(128)}, u32[]{:S(2)}) copy-start(s32[8]{0:T(128)} %param.17) | copy-start | bytes 100
  2.4 39.0 %all-to-all-start = ((bf16[64,40,128]{2,1,0:T(8,128)(2,1)}), bf16[64,40,128]{2,1,0:T(8,128)(2,1)S(1)}, u32[]{:S(2)}, u32[]{:S(2)}) async-start(bf16[64,40,128]{2,1,0:T(8,128)(2,1)} %shard_map.92), calls=%async_computation | async-start | bytes 1310720 | tf_op jit(solution)/shard_map/all_to_all | solution.py:199
  41.5 0.9 copy-start.1
  107.0 3.7 %collective-permute-start = (f32[8,112]{1,0:T(8,128)S(1)}, f32[8,112]{1,0:T(8,128)S(1)}, u32[]{:S(2)}, u32[]{:S(2)}) collective-permute-start(f32[8,112]{1,0:T(8,128)S(1)} %fusion), channel_id=1, source_target_pairs={{0,1},{1,0},{2,3},{3,2},{4,5},{5,4},{6,7},{7,6},{8,9},{9,8},{10,11... | collective-permute-start | bytes 10760 | tf_op jit(solution)/shard_map/ppermute | solution.py:253

commit v2 on v1

v2 whole, which is shorter than its diff:
```python
import functools

import jax
import jax.numpy as jnp
from jax import lax
from jax.experimental import pallas as pl
from jax.experimental.pallas import tpu as pltpu
from jax.sharding import PartitionSpec as P

NEG = -1e30
LANES = 128
GROUP = 4
BATCH = 4
NT = (((1,), (1,)), ((), ()))


def whole(shape):
    return pl.BlockSpec(shape, lambda *_: (0,) * len(shape))


def room(mib):
    return pltpu.CompilerParams(vmem_limit_bytes=mib * 1024 * 1024)


def send_query(q_ref, w_ref, v_ref, out_ref):
    seqs, heads, nope = q_ref.shape
    cols = w_ref.shape[1]
    q = q_ref[...].reshape(seqs * heads, nope)
    w = w_ref[...].reshape(heads * cols, nope)
    every = lax.dot_general(w, q, NT, preferred_element_type=jnp.float32)
    every = every.reshape(heads, cols, seqs * heads)
    head = lax.broadcasted_iota(jnp.int32, every.shape, 0)
    lane = lax.broadcasted_iota(jnp.int32, every.shape, 2)
    part = jnp.sum(jnp.where(lane % heads == head, every, 0.0), axis=0).astype(jnp.bfloat16)
    shards = out_ref.shape[0]
    tiles = seqs * heads // LANES
    for tile in range(tiles):
        piece = part[:, tile * LANES : (tile + 1) * LANES]
        out_ref[:, tile * cols : (tile + 1) * cols, :] = jnp.broadcast_to(piece[None], (shards, cols, LANES))
    out_ref[:, tiles * cols :, :] = v_ref[...]


def order_slots(page_len, first_ref, table_ref, lengths_ref, out_ref, owner_sum, fill_sum):
    seqs, pages = table_ref.shape
    slots = owner_sum.shape[0]
    places = out_ref.shape[1]
    f32, bf16 = jnp.float32, jnp.bfloat16
    logical = lax.broadcasted_iota(jnp.int32, (seqs, pages), 1)
    seq = lax.broadcasted_iota(jnp.int32, (seqs, pages), 0)
    left = lengths_ref[...] - page_len * logical
    local_slot = jnp.where(left > 0, table_ref[...] - first_ref[0], -1)
    tokens = jnp.clip(left, 0, page_len)
    code = (seq * LANES + tokens).astype(f32)

    def at_slot(slot, carry):
        hit = jnp.where(local_slot == slot, code, 0.0)
        acc = hit[:, :LANES]
        for j in range(1, pages // LANES):
            acc = acc + hit[:, j * LANES : (j + 1) * LANES]
        row = jnp.sum(acc, axis=0, keepdims=True)
        owner = jnp.floor(row * (1.0 / LANES))
        owner_sum[pl.ds(slot, 1), :] = owner
        fill_sum[pl.ds(slot, 1), :] = row - owner * LANES
        return carry

    lax.fori_loop(0, slots, at_slot, 0, unroll=4)
    ones = jnp.ones((8, LANES), bf16)
    owner = lax.dot_general(ones, owner_sum[...].astype(bf16), NT, preferred_element_type=f32)
    fill = lax.dot_general(ones, fill_sum[...].astype(bf16), NT, preferred_element_type=f32)

    row = lax.broadcasted_iota(jnp.int32, (seqs, slots), 0)
    slot = lax.broadcasted_iota(jnp.int32, (seqs, slots), 1)
    mine = (owner[:seqs] == row.astype(f32)) & (fill[:seqs] > 0.0)
    ours = jnp.where(mine, 1.0, 0.0)
    before = lax.broadcasted_iota(jnp.int32, (slots, slots), 0) < lax.broadcasted_iota(
        jnp.int32, (slots, slots), 1
    )
    rank = jnp.dot(ours.astype(bf16), jnp.where(before, 1.0, 0.0).astype(bf16), preferred_element_type=f32)
    count = jnp.broadcast_to(jnp.sum(ours, axis=1, keepdims=True), (seqs, slots))
    groups = jnp.floor((count + (GROUP - 1)) * (1.0 / GROUP))
    base, starts = jnp.zeros((1, slots), f32), []
    for b in range(seqs):
        starts.append(base)
        base = base + groups[b : b + 1]
    place = GROUP * jnp.concatenate(starts, axis=0) + rank
    place = jnp.sum(jnp.where(mine, place + 1.0, 0.0), axis=0, keepdims=True) - 1.0
    at = lax.broadcasted_iota(jnp.int32, (places, slots), 0).astype(f32) == place
    value = jnp.where(row == 0, slot.astype(f32), jnp.where(row == 1, fill[:seqs], owner[:seqs]))
    found = lax.dot_general(
        value.astype(bf16), jnp.where(at, 1.0, 0.0).astype(bf16), NT, preferred_element_type=f32
    )
    packed = (found[2:3] * LANES + found[0:1]) * LANES + found[1:2]
    place = lax.broadcasted_iota(jnp.int32, (1, places), 1)
    total = jnp.concatenate([base] * (places // slots), axis=1)
    out_ref[...] = jnp.where(place == places - 1, total, packed).astype(jnp.int32)


def steps_of(order_ref, batch):
    return (order_ref[0, order_ref.shape[1] - 1] + (batch - 1)) // batch


def slot_at(order_ref, group, k):
    code = order_ref[0, GROUP * group + k]
    return (code // LANES) % LANES, code % LANES


def owner_of(order_ref, group):
    return order_ref[0, GROUP * group] // (LANES * LANES)


def score_rope(scale, page_len, order_ref, q_ref, key_ref, out_ref):
    heads = q_ref.shape[1]
    lane = lax.broadcasted_iota(jnp.int32, (heads, GROUP * page_len), 1)

    def score(step, carry):
        for j in range(BATCH):
            group = step * BATCH + j
            keys, limit = [], None
            for k in range(GROUP):
                slot, fill = slot_at(order_ref, group, k)
                keys.append(key_ref[slot])
                end = k * page_len + fill
                limit = end if limit is None else jnp.where(lane >= k * page_len, end, limit)
            keys = jnp.concatenate(keys, axis=0)
            both = lax.dot_general(
                q_ref[owner_of(order_ref, group)], keys, NT, preferred_element_type=jnp.float32
            )
            out_ref[group] = jnp.where(lane < limit, both * scale, NEG)
        return carry

    lax.fori_loop(0, steps_of(order_ref, BATCH), score, 0)


def attend(
    scale, page_len, order_ref, recv_ref, rope_hbm, latent_hbm, out_ref, up_ref,
    latent, query, scores, top, total, acc, rows, sems, rope_sems,
):
    _, tokens, width = latent.shape
    seqs, heads, _ = top.shape
    steps = steps_of(order_ref, BATCH)

    def fetch(step):
        for j in range(BATCH):
            group = step * BATCH + j
            for k in range(GROUP):
                slot, _ = slot_at(order_ref, group, k)
                pltpu.make_async_copy(
                    latent_hbm.at[slot], latent.at[group, pl.ds(k * page_len, page_len)], sems.at[group]
                ).start()
            pltpu.make_async_copy(rope_hbm.at[group], scores.at[group], rope_sems.at[group]).start()

    ahead = 3
    for step in range(ahead):

        @pl.when(step < steps)
        def _():
            fetch(step)

    cols = recv_ref.shape[1] // (seqs * heads // LANES + 1)
    for tile in range(seqs * heads // LANES):
        block = recv_ref[:, tile * cols : (tile + 1) * cols, :].astype(jnp.float32)
        block = block.reshape(width, LANES)
        query[tile * LANES : (tile + 1) * LANES, :] = block.T.astype(jnp.bfloat16)
    up_ref[...] = recv_ref[:, recv_ref.shape[1] - cols :, :]
    top[...] = jnp.full(top.shape, NEG, jnp.float32)
    total[...] = jnp.zeros(total.shape, jnp.float32)
    acc[...] = jnp.zeros(acc.shape, jnp.float32)

    def score(step, carry):
        @pl.when(step + ahead < steps)
        def _():
            fetch(step + ahead)

        for j in range(BATCH):
            group = step * BATCH + j
            pltpu.make_async_copy(latent.at[group], latent.at[group], sems.at[group]).wait()
            pltpu.make_async_copy(rope_hbm.at[group], scores.at[group], rope_sems.at[group]).wait()
        made = []
        for j in range(BATCH):
            group = step * BATCH + j
            b = owner_of(order_ref, group)
            lhs = query[pl.ds(pl.multiple_of(b * heads, heads), heads), :]
            both = lax.dot_general(lhs, latent[group], NT, preferred_element_type=jnp.float32)
            made.append((group, b, both * scale + scores[group]))
        for group, b, both in made:
            scores[group] = both
            high = both[:, :LANES]
            for k in range(1, tokens // LANES):
                high = jnp.maximum(high, both[:, k * LANES : (k + 1) * LANES])
            top[b] = jnp.maximum(top[b], high)
        return carry

    lax.fori_loop(0, steps, score, 0)

    for b in range(seqs):
        top[b] = jnp.broadcast_to(jnp.max(top[b], axis=1, keepdims=True), (heads, LANES))

    def weigh(step, carry):
        made = []
        for j in range(BATCH):
            group = step * BATCH + j
            b = owner_of(order_ref, group)
            both = scores[group]
            peak = top[b]
            parts, some = [], None
            for k in range(tokens // LANES):
                part = both[:, k * LANES : (k + 1) * LANES]
                part = jnp.where(part > 0.5 * NEG, jnp.exp(part - peak), 0.0)
                some = part if some is None else some + part
                parts.append(part.astype(jnp.bfloat16))
            lhs = jnp.concatenate(parts, axis=1)
            made.append((b, some, jnp.dot(lhs, latent[group], preferred_element_type=jnp.float32)))
        for b, some, out in made:
            total[b] = total[b] + some
            acc[b] = acc[b] + out
        return carry

    lax.fori_loop(0, steps, weigh, 0)

    lane = lax.broadcasted_iota(jnp.int32, (heads, LANES), 1)
    for piece in range(width // LANES + 1):
        for b in range(seqs):
            if piece < width // LANES:
                value = acc[b, :, piece * LANES : (piece + 1) * LANES]
            else:
                sums = jnp.broadcast_to(jnp.sum(total[b], axis=1, keepdims=True), (heads, LANES))
                value = jnp.where(lane < 3, top[b], sums)
            rows[piece % 2, pl.ds(b, heads, stride=seqs), :] = value
        value = rows[piece % 2]
        if piece == width // LANES:
            high = value.astype(jnp.bfloat16).astype(jnp.float32)
            middle = (value - high).astype(jnp.bfloat16).astype(jnp.float32)
            low = value - high - middle
            third = lax.broadcasted_iota(jnp.int32, value.shape, 1) % 3
            value = jnp.where(third == 0, high, jnp.where(third == 1, middle, low))
        out_ref[:, :, piece * LANES : (piece + 1) * LANES] = value.reshape(heads, seqs, LANES).astype(jnp.bfloat16)


def combine(width, peers_ref, up_ref, out_ref):
    shards, seqs, _ = peers_ref.shape
    stats = peers_ref[:, :, width:].astype(jnp.float32)
    lane = lax.broadcasted_iota(jnp.int32, stats.shape, 2)
    peak = jnp.sum(jnp.where(lane < 3, stats, 0.0), axis=2, keepdims=True)
    sums = jnp.sum(jnp.where((lane >= 3) & (lane < 6), stats, 0.0), axis=2, keepdims=True)
    rescale = jnp.exp(peak - jnp.max(peak, axis=0, keepdims=True))
    total = jnp.sum(sums * rescale, axis=0)
    mixed = jnp.sum(peers_ref[:, :, :width].astype(jnp.float32) * rescale, axis=0)
    attention = (mixed / total).astype(jnp.bfloat16)
    up = up_ref[...].astype(jnp.float32).reshape(width, up_ref.shape[2]).astype(jnp.bfloat16)
    values = jnp.dot(attention, up, preferred_element_type=jnp.float32).astype(jnp.bfloat16)
    out_ref[...] = jnp.broadcast_to(values[None], out_ref.shape)


def local(
    latent_cache, rope_cache, q_nope, q_rope, w_uk, value_up_weight, w_out, page_table, lengths
):
    slots, page_len, width = latent_cache.shape
    seqs, heads, nope = q_nope.shape
    rope = q_rope.shape[2]
    value_dim = value_up_weight.shape[2]
    cols = w_uk.shape[2]
    shards = lax.axis_size("seq")
    pages = page_table.shape[1]
    scale = (nope + rope) ** -0.5
    f32, bf16 = jnp.float32, jnp.bfloat16

    send_rows = (seqs * heads // LANES + 1) * cols
    sent = pl.pallas_call(
        send_query,
        out_shape=jax.ShapeDtypeStruct((shards, send_rows, LANES), bf16),
        compiler_params=room(8),
    )(q_nope, jnp.swapaxes(w_uk, 1, 2), value_up_weight)
    recv = lax.all_to_all(sent, "seq", 0, 0, tiled=True)

    first = (lax.axis_index("seq") * slots).astype(jnp.int32).reshape(1)
    most = (slots + seqs * (GROUP - 1)) // GROUP
    most = (most + BATCH - 1) // BATCH * BATCH
    places = (most * GROUP) // slots * slots + slots
    smem = pl.BlockSpec(memory_space=pltpu.SMEM)
    order = pl.pallas_call(
        functools.partial(order_slots, page_len),
        out_shape=jax.ShapeDtypeStruct((1, places), jnp.int32),
        in_specs=[smem, whole((seqs, pages)), whole((seqs, 1))],
        scratch_shapes=[pltpu.VMEM((slots, LANES), f32), pltpu.VMEM((slots, LANES), f32)],
        compiler_params=room(4),
    )(first, page_table, lengths.reshape(seqs, 1))
    rope_keys = rope_cache.reshape(slots, page_len, rope)
    tokens = GROUP * page_len
    rope_score = pl.pallas_call(
        functools.partial(score_rope, scale, page_len),
        out_shape=jax.ShapeDtypeStruct((most, heads, tokens), f32),
        in_specs=[smem, whole(q_rope.shape), whole(rope_keys.shape)],
        compiler_params=room(8),
    )(order, q_rope, rope_keys)

    out_width = width + LANES
    partial, up = pl.pallas_call(
        functools.partial(attend, scale, page_len),
        out_shape=(
            jax.ShapeDtypeStruct((heads, seqs, out_width), bf16),
            jax.ShapeDtypeStruct((shards, cols, LANES), bf16),
        ),
        in_specs=[
            smem,
            whole(recv.shape),
            pl.BlockSpec(memory_space=pltpu.HBM),
            pl.BlockSpec(memory_space=pltpu.HBM),
        ],
        scratch_shapes=[
            pltpu.VMEM((most, tokens, width), bf16),
            pltpu.VMEM((seqs * heads, width), bf16),
            pltpu.VMEM((most, heads, tokens), f32),
            pltpu.VMEM((seqs, heads, LANES), f32),
            pltpu.VMEM((seqs, heads, LANES), f32),
            pltpu.VMEM((seqs, heads, width), f32),
            pltpu.VMEM((2, seqs * heads, LANES), f32),
            pltpu.SemaphoreType.DMA((most,)),
            pltpu.SemaphoreType.DMA((most,)),
        ],
        compiler_params=room(52),
    )(order, recv, rope_score, latent_cache)
    peers = lax.all_to_all(partial, "seq", 0, 0, tiled=True)

    values = pl.pallas_call(
        functools.partial(combine, width),
        out_shape=jax.ShapeDtypeStruct((shards, seqs, value_dim), bf16),
        compiler_params=room(8),
    )(peers, up)
    every = lax.all_to_all(values, "seq", 0, 0, tiled=True)
    flat = jnp.swapaxes(every, 0, 1).reshape(seqs, heads * value_dim)
    half = jnp.dot(flat, w_out, preferred_element_type=f32)
    both = half + lax.ppermute(half, "mp", [(0, 1), (1, 0)])
    share = half.shape[1] // lax.axis_size("mp")
    return lax.dynamic_slice_in_dim(both, lax.axis_index("mp") * share, share, 1).astype(bf16)


def solution(mesh):
    return jax.shard_map(
        local,
        mesh=mesh,
        in_specs=(
            P(("groups", "seq"), None, None),
            P(("groups", "seq"), None),
            P("groups", "mp", None),
            P("groups", "mp", None),
            P("mp", None, "seq"),
            P("mp", "seq", None),
            P("mp", "seq"),
            P("groups", None),
            P("groups"),
        ),
        out_specs=P("groups", ("seq", "mp")),
        check_vma=False,
    )
```

time: 112 us -> 106 us (0.946)
  Pallas kernels: 23.2 us -> 17.5 us
  local copies, waits for them, and re-layouts: 7.58 us -> 12.8 us
  waiting for transfers between devices: 9.73 us -> 4.51 us
    all_to_all x1, waiting for transfers between devices: 8.9 us -> 3.69 us  [local(): recv = lax.all_to_all(sent, 'seq', 0, 0, tiled=True)]
    unnamed x7 -> x21, local copies, waits for them, and re-layouts: 2.47 us -> 7.27 us
    pallas_call x2 -> x3, Pallas kernels: 18.7 us -> 15.8 us  [the longest x1 10.8 us: local(): pl.pallas_call(functools.partial(attend, scale, page_len), out_shape=(jax...]
    pallas_call x1, Pallas kernels: 2.18 us -> 0.44 us  [local(): pl.pallas_call(functools.partial(combine, width), out_shape=jax.ShapeDtyp...]
    pallas_call x1, Pallas kernels: 2.4 us -> 1.2 us  [local(): pl.pallas_call(send_query, out_shape=jax.ShapeDtypeStruct((shards, send_r...]
  transfers between devices with their start and end apart: 2 -> 2, of which waited for: 2 -> 2; matrix products, arithmetic and copies ran while one was open for 5% -> 6% of each run, Pallas kernels for 3% -> 5%
where the time goes in v2:
time: 106 us; the launch traced here: 105 us
  blocking collectives  46.2 us (44%)
  starting transfers between devices  23.8 us (22%)
  Pallas kernels  17.5 us (17%)
  local copies, waits for them, and re-layouts  12.8 us (12%)
  waiting for transfers between devices  4.51 us (4%)
    all_to_all x1, blocking collectives, local(): peers = lax.all_to_all(partial, 'seq', 0, 0, tiled=True)  26.9 us
    all_to_all x1, starting transfers between devices, local(): recv = lax.all_to_all(sent, 'seq', 0, 0, tiled=True)  21 us
    all_to_all x1, blocking collectives, local(): every = lax.all_to_all(values, 'seq', 0, 0, tiled=True)  19.3 us
    pallas_call x1, Pallas kernels, local(): pl.pallas_call(functools.partial(attend, scale, page_len), out_shape=(jax...  10.8 us
    unnamed x21, local copies, waits for them, and re-layouts  7.27 us
    reshape x1, local copies, waits for them, and re-layouts, local(): rope_keys = rope_cache.reshape(slots, page_len, rope)  4.77 us
    all_to_all x1, waiting for transfers between devices, local(): recv = lax.all_to_all(sent, 'seq', 0, 0, tiled=True)  3.69 us
    pallas_call x1, Pallas kernels, local(): pl.pallas_call(functools.partial(score_rope, scale, page_len), out_shape=...  3.13 us
  transfers between devices with their start and end apart: 2, of which 2 were waited for; matrix products, arithmetic and copies ran while one was open for 6% of the time, Pallas kernels for 5%

profile of v2, /device:TPU:641, one launch (start us, length us, event | category | flops | bytes accessed | tf_op | source)
XLA Modules:
  0.0 105.4 jit_solution(4584292274370495467)
XLA Ops:
  0.0 0.0 copy-start
  0.0 0.0 copy-start.9
  0.0 0.0 copy-start.3
  0.0 1.0 copy-done.3
  1.1 0.0 copy-start.4
  1.1 0.9 copy-done.4
  2.0 0.0 copy-start.5
  2.0 0.9 copy-done.5
  2.9 0.0 copy-start.8
  2.9 1.2 %shard_map.92 = bf16[64,40,128]{2,1,0:T(8,128)(2,1)} custom-call(bf16[8,64,128]{2,1,0:T(8,128)(2,1)S(1)} %copy-done.3, bf16[64,8,128]{2,1,0:T(8,128)(2,1)S(1)} %bitcast.10, bf16[64,8,128]{2,1,0:T(8,128)(2,1)S(1)} %copy-done.5), custom_call_target="tpu_custom_call" | custom-call | tf_op jit(solution)/shard_map/pallas_call | solution.py:268
  4.1 21.0 %all-to-all-start = ((bf16[64,40,128]{2,1,0:T(8,128)(2,1)}), bf16[64,40,128]{2,1,0:T(8,128)(2,1)S(1)}, u32[]{:S(2)}, u32[]{:S(2)}) async-start(bf16[64,40,128]{2,1,0:T(8,128)(2,1)} %shard_map.92), calls=%async_computation | async-start | bytes 1310720 | tf_op jit(solution)/shard_map/all_to_all | solution.py:273
  25.1 0.0 copy-done.9
  25.1 0.1 copy.11.lengths_ref
  25.2 0.0 copy-done.8
  25.2 1.3 %copy.12 = bf16[128,4096]{0,1:T(8,128)(2,1)} copy(bf16[128,4096]{1,0:T(8,128)(2,1)S(1)} %copy-done.8) | data formatting | bytes 2097152 | tf_op args[1]
  26.5 0.0 copy-start.7
  26.5 0.0 copy-start.6
  26.5 4.8 %copy.13.key_ref = bf16[128,64,64]{2,1,0:T(8,128)(2,1)} copy(bf16[128,64,64]{0,2,1:T(8,128)(2,1)} %bitcast.11) | data formatting | bytes 2097152 | tf_op jit(solution)/shard_map/reshape | solution.py:287
  31.2 0.0 copy-done.7
  31.2 1.9 %shard_map.91.order_ref = s32[1,256]{1,0:T(1,128)S(1)} custom-call(s32[1]{0:T(128)} %bitcast.first_ref, s32[8,2048]{1,0:T(8,128)S(1)} %copy-done.7, s32[8,1]{1,0:T(8,128)S(1)} %copy.11.lengths_ref), custom_call_target="tpu_custom_call" | custom-call | tf_op jit(solution)/shard_map/pallas_call | solution.py:280
  33.2 0.0 copy-done.6
  33.2 0.0 copy-start.2
  33.2 1.6 %copy-done.2 = bf16[128,64,64]{2,1,0:T(8,128)(2,1)S(1)} copy-done((bf16[128,64,64]{2,1,0:T(8,128)(2,1)S(1)}, bf16[128,64,64]{2,1,0:T(8,128)(2,1)}, u32[]{:S(2)}) %copy-start.2) | copy-done | bytes 1048600
  34.8 3.1 %shard_map.93.rope_hbm = f32[40,64,256]{2,1,0:T(8,128)S(1)} custom-call(s32[1,256]{1,0:T(1,128)S(1)} %shard_map.91.order_ref, bf16[8,64,64]{2,1,0:T(8,128)(2,1)S(1)} %copy-done.6, bf16[128,64,64]{2,1,0:T(8,128)(2,1)S(1)} %copy-done.2), custom_call_target="tpu_custom_call" | custom-call | tf_op jit(solution)/shard_map/pallas_call | solution.py:289
  37.9 0.0 copy-start.1
  37.9 1.5 %copy-done.1 = f32[40,64,256]{2,1,0:T(8,128)} copy-done((f32[40,64,256]{2,1,0:T(8,128)}, f32[40,64,256]{2,1,0:T(8,128)S(1)}, u32[]{:S(2)}) %copy-start.1) | copy-done | bytes 2621464
  39.4 3.7 %all-to-all-done.recv_ref = bf16[64,40,128]{2,1,0:T(8,128)(2,1)S(1)} async-done(((bf16[64,40,128]{2,1,0:T(8,128)(2,1)}), bf16[64,40,128]{2,1,0:T(8,128)(2,1)S(1)}, u32[]{:S(2)}, u32[]{:S(2)}) %all-to-all-start) | async-done | bytes 655392 | tf_op jit(solution)/shard_map/all_to_all | solution.py:273
  43.1 10.8 %shard_map.94 = (bf16[64,8,640]{2,1,0:T(8,128)(2,1)S(1)}, bf16[64,8,128]{2,1,0:T(8,128)(2,1)S(1)}) custom-call(s32[1,256]{1,0:T(1,128)S(1)} %shard_map.91.order_ref, bf16[64,40,128]{2,1,0:T(8,128)(2,1)S(1)} %all-to-all-done.recv_ref, f32[40,64,256]{2,1,0:T(8,128)} %copy-done.1, bf16[128,64,512]{2,1,0:T(8,128)(2,1)} %latent_hbm.1), custom_call_target="tpu_custom_call" | custom-call | tf_op jit(solution)/shard_map/pallas_call | solution.py:297
  53.9 26.9 %all_to_all.15.peers_ref = bf16[64,8,640]{2,1,0:T(8,128)(2,1)S(1)} all-to-all(bf16[64,8,640]{2,1,0:T(8,128)(2,1)S(1)} %get-tuple-element.7), channel_id=1, replica_groups=mesh['groups'=2,'seq'=64,'mp'=2] {'seq'}, dimensions={0} | all-to-all | bytes 1310720 | tf_op jit(solution)/shard_map/all_to_all | solution.py:322
  80.8 0.4 shard_map.95
  81.2 19.3 %all_to_all.16 = bf16[64,8,128]{2,1,0:T(8,128)(2,1)S(1)} all-to-all(bf16[64,8,128]{2,1,0:T(8,128)(2,1)S(1)} %shard_map.95), channel_id=1, replica_groups=mesh['groups'=2,'seq'=64,'mp'=2] {'seq'}, dimensions={0} | all-to-all | bytes 262144 | tf_op jit(solution)/shard_map/all_to_all | solution.py:329
  100.5 0.0 copy-done
  100.5 0.6 fusion
  101.1 2.9 %collective-permute-start = (f32[8,112]{1,0:T(8,128)S(1)}, f32[8,112]{1,0:T(8,128)S(1)}, u32[]{:S(2)}, u32[]{:S(2)}) collective-permute-start(f32[8,112]{1,0:T(8,128)S(1)} %fusion), channel_id=1, source_target_pairs={{0,1},{1,0},{2,3},{3,2},{4,5},{5,4},{6,7},{7,6},{8,9},{9,8},{10,11... | collective-permute-start | bytes 10760 | tf_op jit(solution)/shard_map/ppermute | solution.py:332
  104.0 0.8 collective-permute-done
  104.8 0.7 dynamic-slice_convert_fusion
  (1 shorter events, 0.0 us)
Async XLA Ops:
  0.0 100.5 %copy-start = (bf16[8192,112]{0,1:T(8,128)(2,1)S(1)}, bf16[8192,112]{0,1:T(8,128)(2,1)}, u32[]{:S(2)}) copy-start(bf16[8192,112]{0,1:T(8,128)(2,1)} %param.15) | copy-start | bytes 5505028
  0.0 25.1 %copy-start.9 = (s32[8]{0:T(128)S(1)}, s32[8]{0:T(128)}, u32[]{:S(2)}) copy-start(s32[8]{0:T(128)} %param.17) | copy-start | bytes 100
  0.0 1.1 copy-start.3
  1.1 0.9 copy-start.4
  2.0 0.9 copy-start.5
  2.9 22.3 %copy-start.8 = (bf16[128,4096]{1,0:T(8,128)(2,1)S(1)}, bf16[128,4096]{1,0:T(8,128)(2,1)}, u32[]{:S(2)}) copy-start(bf16[128,4096]{1,0:T(8,128)(2,1)} %param.10) | copy-start | bytes 3145732
  4.1 39.1 %all-to-all-start = ((bf16[64,40,128]{2,1,0:T(8,128)(2,1)}), bf16[64,40,128]{2,1,0:T(8,128)(2,1)S(1)}, u32[]{:S(2)}, u32[]{:S(2)}) async-start(bf16[64,40,128]{2,1,0:T(8,128)(2,1)} %shard_map.92), calls=%async_computation | async-start | bytes 1310720 | tf_op jit(solution)/shard_map/all_to_all | solution.py:273
  26.5 4.8 %copy-start.7 = (s32[8,2048]{1,0:T(8,128)S(1)}, s32[8,2048]{1,0:T(8,128)}, u32[]{:S(2)}) copy-start(s32[8,2048]{1,0:T(8,128)} %table_ref.1) | copy-start | bytes 196612
  26.5 6.7 %copy-start.6 = (bf16[8,64,64]{2,1,0:T(8,128)(2,1)S(1)}, bf16[8,64,64]{2,1,0:T(8,128)(2,1)}, u32[]{:S(2)}) copy-start(bf16[8,64,64]{2,1,0:T(8,128)(2,1)} %q_ref.3) | copy-start | bytes 196612
  33.2 1.6 %copy-start.2 = (bf16[128,64,64]{2,1,0:T(8,128)(2,1)S(1)}, bf16[128,64,64]{2,1,0:T(8,128)(2,1)}, u32[]{:S(2)}) copy-start(bf16[128,64,64]{2,1,0:T(8,128)(2,1)} %copy.13.key_ref) | copy-start | bytes 3145732
  37.9 1.5 %copy-start.1 = (f32[40,64,256]{2,1,0:T(8,128)}, f32[40,64,256]{2,1,0:T(8,128)S(1)}, u32[]{:S(2)}) copy-start(f32[40,64,256]{2,1,0:T(8,128)S(1)} %shard_map.93.rope_hbm) | copy-start | bytes 7864324
  101.1 3.7 %collective-permute-start = (f32[8,112]{1,0:T(8,128)S(1)}, f32[8,112]{1,0:T(8,128)S(1)}, u32[]{:S(2)}, u32[]{:S(2)}) collective-permute-start(f32[8,112]{1,0:T(8,128)S(1)} %fusion), channel_id=1, source_target_pairs={{0,1},{1,0},{2,3},{3,2},{4,5},{5,4},{6,7},{7,6},{8,9},{9,8},{10,11... | collective-permute-start | bytes 10760 | tf_op jit(solution)/shard_map/ppermute | solution.py:332

commit v3 on v2

--- a/solution.py
+++ b/solution.py
@@ -22,9 +22,21 @@
     return pltpu.CompilerParams(vmem_limit_bytes=mib * 1024 * 1024)
 
 
-def send_query(q_ref, w_ref, v_ref, out_ref):
+def hbm(x):
+    return pltpu.with_memory_space_constraint(x, pltpu.HBM)
+
+
+def send_query(q_hbm, w_hbm, v_hbm, out_ref, q_ref, w_ref, v_ref, sems):
     seqs, heads, nope = q_ref.shape
     cols = w_ref.shape[1]
+    moves = [
+        pltpu.make_async_copy(source, target, sems.at[i])
+        for i, (source, target) in enumerate(((q_hbm, q_ref), (w_hbm, w_ref), (v_hbm, v_ref)))
+    ]
+    for move in moves:
+        move.start()
+    for move in moves:
+        move.wait()
     q = q_ref[...].reshape(seqs * heads, nope)
     w = w_ref[...].reshape(heads * cols, nope)
     every = lax.dot_general(w, q, NT, preferred_element_type=jnp.float32)
@@ -40,14 +52,20 @@
     out_ref[:, tiles * cols :, :] = v_ref[...]
 
 
-def order_slots(page_len, first_ref, table_ref, lengths_ref, out_ref, owner_sum, fill_sum):
+def order_slots(page_len, first_ref, lengths_ref, table_hbm, out_ref, table_ref, owner_sum, fill_sum, sem):
     seqs, pages = table_ref.shape
     slots = owner_sum.shape[0]
     places = out_ref.shape[1]
     f32, bf16 = jnp.float32, jnp.bfloat16
     logical = lax.broadcasted_iota(jnp.int32, (seqs, pages), 1)
     seq = lax.broadcasted_iota(jnp.int32, (seqs, pages), 0)
-    left = lengths_ref[...] - page_len * logical
+    move = pltpu.make_async_copy(table_hbm, table_ref, sem)
+    move.start()
+    length = jnp.zeros((seqs, pages), jnp.int32)
+    for b in range(seqs):
+        length = jnp.where(seq == b, lengths_ref[b], length)
+    left = length - page_len * logical
+    move.wait()
     local_slot = jnp.where(left > 0, table_ref[...] - first_ref[0], -1)
     tokens = jnp.clip(left, 0, page_len)
     code = (seq * LANES + tokens).astype(f32)
@@ -95,35 +113,60 @@
     out_ref[...] = jnp.where(place == places - 1, total, packed).astype(jnp.int32)
 
 
+SHIFT = 7
+
+
 def steps_of(order_ref, batch):
     return (order_ref[0, order_ref.shape[1] - 1] + (batch - 1)) // batch
 
 
 def slot_at(order_ref, group, k):
     code = order_ref[0, GROUP * group + k]
-    return (code // LANES) % LANES, code % LANES
+    return lax.shift_right_logical(code, SHIFT) & (LANES - 1), code & (LANES - 1)
 
 
 def owner_of(order_ref, group):
-    return order_ref[0, GROUP * group] // (LANES * LANES)
-
-
-def score_rope(scale, page_len, order_ref, q_ref, key_ref, out_ref):
-    heads = q_ref.shape[1]
+    return lax.shift_right_logical(order_ref[0, GROUP * group], 2 * SHIFT)
+
+
+def score_rope(
+    scale, page_len, order_ref, q_hbm, tiles_hbm, out_ref, q_ref, tiles, flat, spread, keys, sems
+):
+    heads, rope = q_ref.shape[1:]
+    blocks, pairs, _, _ = tiles.shape
+    first = pltpu.make_async_copy(q_hbm, q_ref, sems.at[0])
+    second = pltpu.make_async_copy(tiles_hbm, tiles, sems.at[1])
+    first.start()
+    second.start()
+    first.wait()
+    second.wait()
+    even = lax.broadcasted_iota(jnp.int32, (pairs, LANES), 1) < rope
+
+    def spread_block(block, carry):
+        flat[...] = tiles[block].astype(jnp.float32).reshape(pairs * 8, LANES)
+        for k in range(8):
+            two = flat[pl.ds(k, pairs, stride=8), :]
+            spread[k, pl.ds(0, pairs, stride=2), :] = jnp.where(even, two, 0.0)
+            spread[k, pl.ds(1, pairs, stride=2), :] = jnp.where(even, 0.0, two)
+        keys[pl.ds(block * 8, 8)] = spread[...].astype(jnp.bfloat16)
+        return carry
+
+    lax.fori_loop(0, blocks, spread_block, 0)
     lane = lax.broadcasted_iota(jnp.int32, (heads, GROUP * page_len), 1)
 
     def score(step, carry):
         for j in range(BATCH):
             group = step * BATCH + j
-            keys, limit = [], None
+            rows, limit = [], None
             for k in range(GROUP):
                 slot, fill = slot_at(order_ref, group, k)
-                keys.append(key_ref[slot])
+                rows.append(keys[slot])
                 end = k * page_len + fill
                 limit = end if limit is None else jnp.where(lane >= k * page_len, end, limit)
-            keys = jnp.concatenate(keys, axis=0)
+            query = q_ref[owner_of(order_ref, group)].astype(jnp.float32)
+            query = jnp.concatenate([query, query], axis=1).astype(jnp.bfloat16)
             both = lax.dot_general(
-                q_ref[owner_of(order_ref, group)], keys, NT, preferred_element_type=jnp.float32
+                query, jnp.concatenate(rows, axis=0), NT, preferred_element_type=jnp.float32
             )
             out_ref[group] = jnp.where(lane < limit, both * scale, NEG)
         return carry
@@ -145,9 +188,10 @@
             for k in range(GROUP):
                 slot, _ = slot_at(order_ref, group, k)
                 pltpu.make_async_copy(
-                    latent_hbm.at[slot], latent.at[group, pl.ds(k * page_len, page_len)], sems.at[group]
+                    latent_hbm.at[slot], latent.at[group, pl.ds(k * page_len, page_len)], sems.at[step]
                 ).start()
-            pltpu.make_async_copy(rope_hbm.at[group], scores.at[group], rope_sems.at[group]).start()
+        batch = pl.ds(step * BATCH, BATCH)
+        pltpu.make_async_copy(rope_hbm.at[batch], scores.at[batch], rope_sems.at[step]).start()
 
     ahead = 3
     for step in range(ahead):
@@ -171,10 +215,9 @@
         def _():
             fetch(step + ahead)
 
-        for j in range(BATCH):
-            group = step * BATCH + j
-            pltpu.make_async_copy(latent.at[group], latent.at[group], sems.at[group]).wait()
-            pltpu.make_async_copy(rope_hbm.at[group], scores.at[group], rope_sems.at[group]).wait()
+        batch = pl.ds(step * BATCH, BATCH)
+        pltpu.make_async_copy(latent.at[batch], latent.at[batch], sems.at[step]).wait()
+        pltpu.make_async_copy(rope_hbm.at[batch], scores.at[batch], rope_sems.at[step]).wait()
         made = []
         for j in range(BATCH):
             group = step * BATCH + j
@@ -267,9 +310,16 @@
     send_rows = (seqs * heads // LANES + 1) * cols
     sent = pl.pallas_call(
         send_query,
+        in_specs=[pl.BlockSpec(memory_space=pltpu.HBM)] * 3,
         out_shape=jax.ShapeDtypeStruct((shards, send_rows, LANES), bf16),
+        scratch_shapes=[
+            pltpu.VMEM(q_nope.shape, bf16),
+            pltpu.VMEM((heads, cols, nope), bf16),
+            pltpu.VMEM(value_up_weight.shape, bf16),
+            pltpu.SemaphoreType.DMA((3,)),
+        ],
         compiler_params=room(8),
-    )(q_nope, jnp.swapaxes(w_uk, 1, 2), value_up_weight)
+    )(hbm(q_nope), hbm(jnp.swapaxes(w_uk, 1, 2)), hbm(value_up_weight))
     recv = lax.all_to_all(sent, "seq", 0, 0, tiled=True)
 
     first = (lax.axis_index("seq") * slots).astype(jnp.int32).reshape(1)
@@ -277,21 +327,36 @@
     most = (most + BATCH - 1) // BATCH * BATCH
     places = (most * GROUP) // slots * slots + slots
     smem = pl.BlockSpec(memory_space=pltpu.SMEM)
+    in_hbm = pl.BlockSpec(memory_space=pltpu.HBM)
     order = pl.pallas_call(
         functools.partial(order_slots, page_len),
         out_shape=jax.ShapeDtypeStruct((1, places), jnp.int32),
-        in_specs=[smem, whole((seqs, pages)), whole((seqs, 1))],
-        scratch_shapes=[pltpu.VMEM((slots, LANES), f32), pltpu.VMEM((slots, LANES), f32)],
+        in_specs=[smem, smem, in_hbm],
+        scratch_shapes=[
+            pltpu.VMEM((seqs, pages), jnp.int32),
+            pltpu.VMEM((slots, LANES), f32),
+            pltpu.VMEM((slots, LANES), f32),
+            pltpu.SemaphoreType.DMA,
+        ],
         compiler_params=room(4),
-    )(first, page_table, lengths.reshape(seqs, 1))
-    rope_keys = rope_cache.reshape(slots, page_len, rope)
+    )(first, lengths, hbm(page_table))
+    rope_tiles = rope_cache.reshape(slots // 8, 8, page_len * rope // LANES, LANES)
+    rope_tiles = jnp.swapaxes(rope_tiles, 1, 2)
     tokens = GROUP * page_len
     rope_score = pl.pallas_call(
         functools.partial(score_rope, scale, page_len),
-        out_shape=jax.ShapeDtypeStruct((most, heads, tokens), f32),
-        in_specs=[smem, whole(q_rope.shape), whole(rope_keys.shape)],
-        compiler_params=room(8),
-    )(order, q_rope, rope_keys)
+        out_shape=pltpu.HBM((most, heads, tokens), f32),
+        in_specs=[smem, in_hbm, in_hbm],
+        scratch_shapes=[
+            pltpu.VMEM(q_rope.shape, bf16),
+            pltpu.VMEM(rope_tiles.shape, bf16),
+            pltpu.VMEM((page_len * rope * 8 // LANES, LANES), f32),
+            pltpu.VMEM((8, page_len, LANES), f32),
+            pltpu.VMEM((slots, page_len, LANES), bf16),
+            pltpu.SemaphoreType.DMA((2,)),
+        ],
+        compiler_params=room(16),
+    )(order, hbm(q_rope), hbm(rope_tiles))
 
     out_width = width + LANES
     partial, up = pl.pallas_call(
@@ -303,8 +368,8 @@
         in_specs=[
             smem,
             whole(recv.shape),
-            pl.BlockSpec(memory_space=pltpu.HBM),
-            pl.BlockSpec(memory_space=pltpu.HBM),
+            in_hbm,
+            in_hbm,
         ],
         scratch_shapes=[
             pltpu.VMEM((most, tokens, width), bf16),
@@ -314,11 +379,11 @@
             pltpu.VMEM((seqs, heads, LANES), f32),
             pltpu.VMEM((seqs, heads, width), f32),
             pltpu.VMEM((2, seqs * heads, LANES), f32),
-            pltpu.SemaphoreType.DMA((most,)),
-            pltpu.SemaphoreType.DMA((most,)),
+            pltpu.SemaphoreType.DMA((most // BATCH,)),
+            pltpu.SemaphoreType.DMA((most // BATCH,)),
         ],
-        compiler_params=room(52),
-    )(order, recv, rope_score, latent_cache)
+        compiler_params=room(24),
+    )(order, recv, hbm(rope_score), hbm(latent_cache))
     peers = lax.all_to_all(partial, "seq", 0, 0, tiled=True)
 
     values = pl.pallas_call(

time: 106 us -> 103 us (0.972)
  local copies, waits for them, and re-layouts: 12.8 us -> 0.66 us
  blocking collectives: 46.2 us -> 54.3 us
  waiting for transfers between devices: 4.51 us -> 11.3 us
  Pallas kernels: 17.5 us -> 12.1 us
    pallas_call x1, Pallas kernels: 10.8 us -> 1.63 us  [local(): pl.pallas_call(functools.partial(attend, scale, page_len), out_shape=(jax...]
    all_to_all x1, blocking collectives: 26.9 us -> 34.5 us  [local(): peers = lax.all_to_all(partial, 'seq', 0, 0, tiled=True)]
    unnamed x21 -> x4, local copies, waits for them, and re-layouts: 7.27 us -> 0.01 us
    all_to_all x1, waiting for transfers between devices: 3.69 us -> 10.4 us  [local(): recv = lax.all_to_all(sent, 'seq', 0, 0, tiled=True)]
    reshape x2 -> x0, local copies, waits for them, and re-layouts: 4.85 us -> none  [the longest x1 4.77 us: local(): rope_keys = rope_cache.reshape(slots, page_len, rope)]
    pallas_call x1, Pallas kernels: 1.93 us -> 3.26 us  [local(): pl.pallas_call(functools.partial(order_slots, page_len), out_shape=jax.Sh...]
    pallas_call x1, Pallas kernels: 3.13 us -> 4.35 us  [local(): pl.pallas_call(functools.partial(score_rope, scale, page_len), out_shape=...]
    pallas_call x1, Pallas kernels: 1.2 us -> 2.41 us  [local(): pl.pallas_call(send_query, in_specs=[pl.BlockSpec(memory_space=pltpu.HBM)...]
  transfers between devices with their start and end apart: 2 -> 2, of which waited for: 2 -> 2; matrix products, arithmetic and copies ran while one was open for 6% -> 0% of each run, Pallas kernels for 5% -> 7%
where the time goes in v3:
time: 103 us
  blocking collectives  54.3 us (53%)
  starting transfers between devices  23.9 us (23%)
  Pallas kernels  12.1 us (12%)
  waiting for transfers between devices  11.3 us (11%)
    all_to_all x1, blocking collectives, local(): peers = lax.all_to_all(partial, 'seq', 0, 0, tiled=True)  34.5 us
    all_to_all x1, starting transfers between devices, local(): recv = lax.all_to_all(sent, 'seq', 0, 0, tiled=True)  21 us
    all_to_all x1, blocking collectives, local(): every = lax.all_to_all(values, 'seq', 0, 0, tiled=True)  19.8 us
    all_to_all x1, waiting for transfers between devices, local(): recv = lax.all_to_all(sent, 'seq', 0, 0, tiled=True)  10.4 us
    pallas_call x1, Pallas kernels, local(): pl.pallas_call(functools.partial(score_rope, scale, page_len), out_shape=...  4.35 us
    pallas_call x1, Pallas kernels, local(): pl.pallas_call(functools.partial(order_slots, page_len), out_shape=jax.Sh...  3.26 us
    ppermute x1, starting transfers between devices, local(): both = half + lax.ppermute(half, 'mp', [(0, 1), (1, 0)])  2.9 us
    pallas_call x1, Pallas kernels, local(): pl.pallas_call(send_query, in_specs=[pl.BlockSpec(memory_space=pltpu.HBM)...  2.41 us
  transfers between devices with their start and end apart: 2, of which 2 were waited for; matrix products, arithmetic and copies ran while one was open for 0% of the time, Pallas kernels for 7%

profile of v3, /device:TPU:641, one launch (start us, length us, event | category | flops | bytes accessed | tf_op | source)
XLA Modules:
  0.0 102.8 jit_solution(15972093642081907242)
XLA Ops:
  0.0 0.0 copy-start
  0.0 0.0 copy-start.1
  0.0 2.4 %shard_map.92 = bf16[64,40,128]{2,1,0:T(8,128)(2,1)} custom-call(bf16[8,64,128]{2,1,0:T(8,128)(2,1)} %q_hbm.2, bf16[64,8,128]{2,1,0:T(8,128)(2,1)} %bitcast.12, bf16[64,8,128]{2,1,0:T(8,128)(2,1)} %v_hbm.1), custom_call_target="tpu_custom_call" | custom-call | tf_op jit(solution)/shard_map/pallas_call | solution.py:311
  2.4 21.0 %all-to-all-start = ((bf16[64,40,128]{2,1,0:T(8,128)(2,1)}), bf16[64,40,128]{2,1,0:T(8,128)(2,1)S(1)}, u32[]{:S(2)}, u32[]{:S(2)}) async-start(bf16[64,40,128]{2,1,0:T(8,128)(2,1)} %shard_map.92), calls=%async_computation | async-start | bytes 1310720 | tf_op jit(solution)/shard_map/all_to_all | solution.py:323
  23.4 0.0 copy-done.1
  23.4 3.3 %shard_map.91.order_ref = s32[1,256]{1,0:T(1,128)S(1)} custom-call(s32[1]{0:T(128)} %bitcast.first_ref, s32[8]{0:T(128)S(1)} %copy-done.1, s32[8,2048]{1,0:T(8,128)} %table_hbm.1), custom_call_target="tpu_custom_call" | custom-call | tf_op jit(solution)/shard_map/pallas_call | solution.py:331
  26.7 4.4 %shard_map.93.rope_hbm = f32[40,64,256]{2,1,0:T(8,128)} custom-call(s32[1,256]{1,0:T(1,128)S(1)} %shard_map.91.order_ref, bf16[8,64,64]{2,1,0:T(8,128)(2,1)} %q_hbm.3, bf16[16,32,8,128]{3,2,1,0:T(8,128)(2,1)} %bitcast.11), custom_call_target="tpu_custom_call" | custom-call | tf_op jit(solution)/shard_map/pallas_call | solution.py:346
  31.1 10.4 %all-to-all-done.recv_ref = bf16[64,40,128]{2,1,0:T(8,128)(2,1)S(1)} async-done(((bf16[64,40,128]{2,1,0:T(8,128)(2,1)}), bf16[64,40,128]{2,1,0:T(8,128)(2,1)S(1)}, u32[]{:S(2)}, u32[]{:S(2)}) %all-to-all-start) | async-done | bytes 655392 | tf_op jit(solution)/shard_map/all_to_all | solution.py:323
  41.5 1.6 %shard_map.94 = (bf16[64,8,640]{2,1,0:T(8,128)(2,1)S(1)}, bf16[64,8,128]{2,1,0:T(8,128)(2,1)S(1)}) custom-call(s32[1,256]{1,0:T(1,128)S(1)} %shard_map.91.order_ref, bf16[64,40,128]{2,1,0:T(8,128)(2,1)S(1)} %all-to-all-done.recv_ref, f32[40,64,256]{2,1,0:T(8,128)} %shard_map.93.rope_hbm, bf16[128,64,512]{2,1,0:T(8,128)(2,1)} %latent_hbm.1), custom_call_target="tpu_custom_call" | custom-call | tf_op jit(solution)/shard_map/pallas_call | solution.py:362
  43.1 34.5 %all_to_all.15.peers_ref = bf16[64,8,640]{2,1,0:T(8,128)(2,1)S(1)} all-to-all(bf16[64,8,640]{2,1,0:T(8,128)(2,1)S(1)} %get-tuple-element.7), channel_id=1, replica_groups=mesh['groups'=2,'seq'=64,'mp'=2] {'seq'}, dimensions={0} | all-to-all | bytes 1310720 | tf_op jit(solution)/shard_map/all_to_all | solution.py:387
  77.6 0.4 shard_map.95
  78.0 19.8 %all_to_all.16 = bf16[64,8,128]{2,1,0:T(8,128)(2,1)S(1)} all-to-all(bf16[64,8,128]{2,1,0:T(8,128)(2,1)S(1)} %shard_map.95), channel_id=1, replica_groups=mesh['groups'=2,'seq'=64,'mp'=2] {'seq'}, dimensions={0} | all-to-all | bytes 262144 | tf_op jit(solution)/shard_map/all_to_all | solution.py:394
  97.9 0.0 copy-done
  97.9 0.6 fusion
  98.4 2.9 %collective-permute-start = (f32[8,112]{1,0:T(8,128)S(1)}, f32[8,112]{1,0:T(8,128)S(1)}, u32[]{:S(2)}, u32[]{:S(2)}) collective-permute-start(f32[8,112]{1,0:T(8,128)S(1)} %fusion), channel_id=1, source_target_pairs={{0,1},{1,0},{2,3},{3,2},{4,5},{5,4},{6,7},{7,6},{8,9},{9,8},{10,11... | collective-permute-start | bytes 10760 | tf_op jit(solution)/shard_map/ppermute | solution.py:397
  101.3 0.8 collective-permute-done
  102.2 0.7 dynamic-slice_convert_fusion
  (1 shorter events, 0.0 us)
Async XLA Ops:
  0.0 97.9 %copy-start = (bf16[8192,112]{0,1:T(8,128)(2,1)S(1)}, bf16[8192,112]{0,1:T(8,128)(2,1)}, u32[]{:S(2)}) copy-start(bf16[8192,112]{0,1:T(8,128)(2,1)} %param.15) | copy-start | bytes 5505028
  0.0 23.4 %copy-start.1 = (s32[8]{0:T(128)S(1)}, s32[8]{0:T(128)}, u32[]{:S(2)}) copy-start(s32[8]{0:T(128)} %lengths_ref.1) | copy-start | bytes 100
  2.4 39.1 %all-to-all-start = ((bf16[64,40,128]{2,1,0:T(8,128)(2,1)}), bf16[64,40,128]{2,1,0:T(8,128)(2,1)S(1)}, u32[]{:S(2)}, u32[]{:S(2)}) async-start(bf16[64,40,128]{2,1,0:T(8,128)(2,1)} %shard_map.92), calls=%async_computation | async-start | bytes 1310720 | tf_op jit(solution)/shard_map/all_to_all | solution.py:323
  98.4 3.7 %collective-permute-start = (f32[8,112]{1,0:T(8,128)S(1)}, f32[8,112]{1,0:T(8,128)S(1)}, u32[]{:S(2)}, u32[]{:S(2)}) collective-permute-start(f32[8,112]{1,0:T(8,128)S(1)} %fusion), channel_id=1, source_target_pairs={{0,1},{1,0},{2,3},{3,2},{4,5},{5,4},{6,7},{7,6},{8,9},{9,8},{10,11... | collective-permute-start | bytes 10760 | tf_op jit(solution)/shard_map/ppermute | solution.py:397

commit v4 on v3

--- a/solution.py
+++ b/solution.py
@@ -5,6 +5,7 @@
 from jax import lax
 from jax.experimental import pallas as pl
 from jax.experimental.pallas import tpu as pltpu
+from jax.sharding import Mesh
 from jax.sharding import PartitionSpec as P
 
 NEG = -1e30
@@ -175,7 +176,7 @@
 
 
 def attend(
-    scale, page_len, order_ref, recv_ref, rope_hbm, latent_hbm, out_ref, up_ref,
+    scale, page_len, sender, order_ref, recv_ref, rope_hbm, latent_hbm, out_ref, up_ref,
     latent, query, scores, top, total, acc, rows, sems, rope_sems,
 ):
     _, tokens, width = latent.shape
@@ -203,9 +204,10 @@
     cols = recv_ref.shape[1] // (seqs * heads // LANES + 1)
     for tile in range(seqs * heads // LANES):
         block = recv_ref[:, tile * cols : (tile + 1) * cols, :].astype(jnp.float32)
-        block = block.reshape(width, LANES)
+        block = jnp.concatenate([block[at] for at in sender], axis=0)
         query[tile * LANES : (tile + 1) * LANES, :] = block.T.astype(jnp.bfloat16)
-    up_ref[...] = recv_ref[:, recv_ref.shape[1] - cols :, :]
+    for shard, at in enumerate(sender):
+        up_ref[shard] = recv_ref[at, recv_ref.shape[1] - cols :, :]
     top[...] = jnp.full(top.shape, NEG, jnp.float32)
     total[...] = jnp.zeros(total.shape, jnp.float32)
     acc[...] = jnp.zeros(acc.shape, jnp.float32)
@@ -295,14 +297,15 @@
 
 
 def local(
-    latent_cache, rope_cache, q_nope, q_rope, w_uk, value_up_weight, w_out, page_table, lengths
+    seq, peers_order,
+    latent_cache, rope_cache, q_nope, q_rope, w_uk, value_up_weight, w_out, page_table, lengths,
 ):
     slots, page_len, width = latent_cache.shape
     seqs, heads, nope = q_nope.shape
     rope = q_rope.shape[2]
     value_dim = value_up_weight.shape[2]
     cols = w_uk.shape[2]
-    shards = lax.axis_size("seq")
+    shards = lax.axis_size(seq)
     pages = page_table.shape[1]
     scale = (nope + rope) ** -0.5
     f32, bf16 = jnp.float32, jnp.bfloat16
@@ -320,9 +323,9 @@
         ],
         compiler_params=room(8),
     )(hbm(q_nope), hbm(jnp.swapaxes(w_uk, 1, 2)), hbm(value_up_weight))
-    recv = lax.all_to_all(sent, "seq", 0, 0, tiled=True)
-
-    first = (lax.axis_index("seq") * slots).astype(jnp.int32).reshape(1)
+    recv = lax.all_to_all(sent, peers_order, 0, 0, tiled=True)
+
+    first = (lax.axis_index(seq) * slots).astype(jnp.int32).reshape(1)
     most = (slots + seqs * (GROUP - 1)) // GROUP
     most = (most + BATCH - 1) // BATCH * BATCH
     places = (most * GROUP) // slots * slots + slots
@@ -360,7 +363,7 @@
 
     out_width = width + LANES
     partial, up = pl.pallas_call(
-        functools.partial(attend, scale, page_len),
+        functools.partial(attend, scale, page_len, sender_of(seq, peers_order)),
         out_shape=(
             jax.ShapeDtypeStruct((heads, seqs, out_width), bf16),
             jax.ShapeDtypeStruct((shards, cols, LANES), bf16),
@@ -384,14 +387,14 @@
         ],
         compiler_params=room(24),
     )(order, recv, hbm(rope_score), hbm(latent_cache))
-    peers = lax.all_to_all(partial, "seq", 0, 0, tiled=True)
+    peers = lax.all_to_all(partial, peers_order, 0, 0, tiled=True)
 
     values = pl.pallas_call(
         functools.partial(combine, width),
         out_shape=jax.ShapeDtypeStruct((shards, seqs, value_dim), bf16),
         compiler_params=room(8),
     )(peers, up)
-    every = lax.all_to_all(values, "seq", 0, 0, tiled=True)
+    every = lax.all_to_all(values, peers_order, 0, 0, tiled=True)
     flat = jnp.swapaxes(every, 0, 1).reshape(seqs, heads * value_dim)
     half = jnp.dot(flat, w_out, preferred_element_type=f32)
     both = half + lax.ppermute(half, "mp", [(0, 1), (1, 0)])
@@ -399,21 +402,38 @@
     return lax.dynamic_slice_in_dim(both, lax.axis_index("mp") * share, share, 1).astype(bf16)
 
 
+def sender_of(seq, peers_order):
+    bits = len(seq)
+    places = []
+    for shard in range(2**bits):
+        bit = {axis: shard >> (bits - 1 - i) & 1 for i, axis in enumerate(seq)}
+        places.append(sum(bit[axis] << (bits - 1 - i) for i, axis in enumerate(peers_order)))
+    return tuple(places)
+
+
 def solution(mesh):
+    bits = mesh.shape["seq"].bit_length() - 1
+    assert mesh.shape["seq"] == 2**bits and bits % 2 == 0
+    seq = tuple(f"seq_{i}" for i in range(bits))
+    peers_order = tuple(axis for both in zip(seq[: bits // 2], seq[bits // 2 :]) for axis in both)
+    finer = Mesh(
+        mesh.devices.reshape(mesh.shape["groups"], *(2,) * bits, mesh.shape["mp"]),
+        ("groups", *seq, "mp"),
+    )
     return jax.shard_map(
-        local,
-        mesh=mesh,
+        functools.partial(local, seq, peers_order),
+        mesh=finer,
         in_specs=(
-            P(("groups", "seq"), None, None),
-            P(("groups", "seq"), None),
+            P(("groups", *seq), None, None),
+            P(("groups", *seq), None),
             P("groups", "mp", None),
             P("groups", "mp", None),
-            P("mp", None, "seq"),
-            P("mp", "seq", None),
-            P("mp", "seq"),
+            P("mp", None, seq),
+            P("mp", seq, None),
+            P("mp", seq),
             P("groups", None),
             P("groups"),
         ),
-        out_specs=P("groups", ("seq", "mp")),
+        out_specs=P("groups", (*seq, "mp")),
         check_vma=False,
     )

time: 103 us -> 104 us (level)
  Pallas kernels: 12.1 us -> 15.2 us
    pallas_call x1, Pallas kernels: 1.63 us -> 4.22 us  [local(): pl.pallas_call(functools.partial(attend, scale, page_len, sender_of(seq,...]
  transfers between devices with their start and end apart: 2 -> 2, of which waited for: 2 -> 2; matrix products, arithmetic and copies ran while one was open for 0% -> 0% of each run, Pallas kernels for 7% -> 8%
where the time goes in v4:
time: 104 us; the launch traced here: 105 us
  blocking collectives  53.4 us (51%)
  starting transfers between devices  23.6 us (23%)
  Pallas kernels  15.2 us (15%)
  waiting for transfers between devices  11.3 us (11%)
    all_to_all x1, blocking collectives, local(): peers = lax.all_to_all(partial, peers_order, 0, 0, tiled=True)  33 us
    all_to_all x1, starting transfers between devices, local(): recv = lax.all_to_all(sent, peers_order, 0, 0, tiled=True)  21 us
    all_to_all x1, blocking collectives, local(): every = lax.all_to_all(values, peers_order, 0, 0, tiled=True)  20.4 us
    all_to_all x1, waiting for transfers between devices, local(): recv = lax.all_to_all(sent, peers_order, 0, 0, tiled=True)  10.5 us
    pallas_call x1, Pallas kernels, local(): pl.pallas_call(functools.partial(score_rope, scale, page_len), out_shape=...  4.86 us
    pallas_call x1, Pallas kernels, local(): pl.pallas_call(functools.partial(attend, scale, page_len, sender_of(seq,...  4.22 us
    pallas_call x1, Pallas kernels, local(): pl.pallas_call(functools.partial(order_slots, page_len), out_shape=jax.Sh...  3.26 us
    ppermute x1, starting transfers between devices, local(): both = half + lax.ppermute(half, 'mp', [(0, 1), (1, 0)])  2.57 us
  transfers between devices with their start and end apart: 2, of which 2 were waited for; matrix products, arithmetic and copies ran while one was open for 0% of the time, Pallas kernels for 8%

profile of v4, /device:TPU:641, one launch (start us, length us, event | category | flops | bytes accessed | tf_op | source)
XLA Modules:
  0.0 104.8 jit_solution(9494944809594820171)
XLA Ops:
  0.0 0.0 copy-start
  0.0 0.0 copy-start.1
  0.0 2.4 %shard_map.92 = bf16[64,40,128]{2,1,0:T(8,128)(2,1)} custom-call(bf16[8,64,128]{2,1,0:T(8,128)(2,1)} %q_hbm.2, bf16[64,8,128]{2,1,0:T(8,128)(2,1)} %bitcast.12, bf16[64,8,128]{2,1,0:T(8,128)(2,1)} %v_hbm.1), custom_call_target="tpu_custom_call" | custom-call | tf_op jit(solution)/shard_map/pallas_call | solution.py:314
  2.4 21.0 %all-to-all-start = ((bf16[64,40,128]{2,1,0:T(8,128)(2,1)}), bf16[64,40,128]{2,1,0:T(8,128)(2,1)S(1)}, u32[]{:S(2)}, u32[]{:S(2)}) async-start(bf16[64,40,128]{2,1,0:T(8,128)(2,1)} %shard_map.92), calls=%async_computation | async-start | bytes 1310720 | tf_op jit(solution)/shard_map/all_to_all | solution.py:326
  23.4 0.0 copy-done.1
  23.4 3.3 %shard_map.91.order_ref = s32[1,256]{1,0:T(1,128)S(1)} custom-call(s32[1]{0:T(128)} %bitcast.first_ref, s32[8]{0:T(128)S(1)} %copy-done.1, s32[8,2048]{1,0:T(8,128)} %table_hbm.1), custom_call_target="tpu_custom_call" | custom-call | tf_op jit(solution)/shard_map/pallas_call | solution.py:334
  26.7 4.9 %shard_map.93.rope_hbm = f32[40,64,256]{2,1,0:T(8,128)} custom-call(s32[1,256]{1,0:T(1,128)S(1)} %shard_map.91.order_ref, bf16[8,64,64]{2,1,0:T(8,128)(2,1)} %q_hbm.3, bf16[16,32,8,128]{3,2,1,0:T(8,128)(2,1)} %bitcast.11), custom_call_target="tpu_custom_call" | custom-call | tf_op jit(solution)/shard_map/pallas_call | solution.py:349
  31.6 10.5 %all-to-all-done.recv_ref = bf16[64,40,128]{2,1,0:T(8,128)(2,1)S(1)} async-done(((bf16[64,40,128]{2,1,0:T(8,128)(2,1)}), bf16[64,40,128]{2,1,0:T(8,128)(2,1)S(1)}, u32[]{:S(2)}, u32[]{:S(2)}) %all-to-all-start) | async-done | bytes 655392 | tf_op jit(solution)/shard_map/all_to_all | solution.py:326
  42.0 4.2 %shard_map.94 = (bf16[64,8,640]{2,1,0:T(8,128)(2,1)S(1)}, bf16[64,8,128]{2,1,0:T(8,128)(2,1)S(1)}) custom-call(s32[1,256]{1,0:T(1,128)S(1)} %shard_map.91.order_ref, bf16[64,40,128]{2,1,0:T(8,128)(2,1)S(1)} %all-to-all-done.recv_ref, f32[40,64,256]{2,1,0:T(8,128)} %shard_map.93.rope_hbm, bf16[128,64,512]{2,1,0:T(8,128)(2,1)} %latent_hbm.1), custom_call_target="tpu_custom_call" | custom-call | tf_op jit(solution)/shard_map/pallas_call | solution.py:365
  46.3 33.0 %all_to_all.15.peers_ref = bf16[64,8,640]{2,1,0:T(8,128)(2,1)S(1)} all-to-all(bf16[64,8,640]{2,1,0:T(8,128)(2,1)S(1)} %get-tuple-element.7), channel_id=1, replica_groups=mesh['groups'=2,'seq_0'=2,'seq_1'=2,'seq_2'=2,'seq_3'=2,'seq_4'=2,'seq_5..., dimensions={0} | all-to-all | bytes 1310720 | tf_op jit(solution)/shard_map/all_to_all | solution.py:390
  79.3 0.4 shard_map.95
  79.8 20.4 %all_to_all.16 = bf16[64,8,128]{2,1,0:T(8,128)(2,1)S(1)} all-to-all(bf16[64,8,128]{2,1,0:T(8,128)(2,1)S(1)} %shard_map.95), channel_id=1, replica_groups=mesh['groups'=2,'seq_0'=2,'seq_1'=2,'seq_2'=2,'seq_3'=2,'seq_4'=2,'seq_5..., dimensions={0} | all-to-all | bytes 262144 | tf_op jit(solution)/shard_map/all_to_all | solution.py:397
  100.2 0.0 copy-done
  100.2 0.6 fusion
  100.7 2.6 %collective-permute-start = (f32[8,112]{1,0:T(8,128)S(1)}, f32[8,112]{1,0:T(8,128)S(1)}, u32[]{:S(2)}, u32[]{:S(2)}) collective-permute-start(f32[8,112]{1,0:T(8,128)S(1)} %fusion), channel_id=1, source_target_pairs={{0,1},{1,0},{2,3},{3,2},{4,5},{5,4},{6,7},{7,6},{8,9},{9,8},{10,11... | collective-permute-start | bytes 10760 | tf_op jit(solution)/shard_map/ppermute | solution.py:400
  103.3 0.8 collective-permute-done
  104.1 0.7 dynamic-slice_convert_fusion
  (1 shorter events, 0.0 us)
Async XLA Ops:
  0.0 100.2 %copy-start = (bf16[8192,112]{0,1:T(8,128)(2,1)S(1)}, bf16[8192,112]{0,1:T(8,128)(2,1)}, u32[]{:S(2)}) copy-start(bf16[8192,112]{0,1:T(8,128)(2,1)} %param.15) | copy-start | bytes 5505028
  0.0 23.4 %copy-start.1 = (s32[8]{0:T(128)S(1)}, s32[8]{0:T(128)}, u32[]{:S(2)}) copy-start(s32[8]{0:T(128)} %lengths_ref.1) | copy-start | bytes 100
  2.4 39.6 %all-to-all-start = ((bf16[64,40,128]{2,1,0:T(8,128)(2,1)}), bf16[64,40,128]{2,1,0:T(8,128)(2,1)S(1)}, u32[]{:S(2)}, u32[]{:S(2)}) async-start(bf16[64,40,128]{2,1,0:T(8,128)(2,1)} %shard_map.92), calls=%async_computation | async-start | bytes 1310720 | tf_op jit(solution)/shard_map/all_to_all | solution.py:326
  100.7 3.4 %collective-permute-start = (f32[8,112]{1,0:T(8,128)S(1)}, f32[8,112]{1,0:T(8,128)S(1)}, u32[]{:S(2)}, u32[]{:S(2)}) collective-permute-start(f32[8,112]{1,0:T(8,128)S(1)} %fusion), channel_id=1, source_target_pairs={{0,1},{1,0},{2,3},{3,2},{4,5},{5,4},{6,7},{7,6},{8,9},{9,8},{10,11... | collective-permute-start | bytes 10760 | tf_op jit(solution)/shard_map/ppermute | solution.py:400

commit v5 on v4

--- a/solution.py
+++ b/solution.py
@@ -415,7 +415,7 @@
     bits = mesh.shape["seq"].bit_length() - 1
     assert mesh.shape["seq"] == 2**bits and bits % 2 == 0
     seq = tuple(f"seq_{i}" for i in range(bits))
-    peers_order = tuple(axis for both in zip(seq[: bits // 2], seq[bits // 2 :]) for axis in both)
+    peers_order = seq[: bits // 2][::-1] + seq[bits // 2 :][::-1]
     finer = Mesh(
         mesh.devices.reshape(mesh.shape["groups"], *(2,) * bits, mesh.shape["mp"]),
         ("groups", *seq, "mp"),

time: 104 us -> 103 us (level); the launches traced: 105 us -> 102 us
  Pallas kernels: 15.2 us -> 12.1 us
  waiting for transfers between devices: 11.3 us -> 13.4 us
  blocking collectives: 53.4 us -> 51.4 us
    all_to_all x1, blocking collectives: 20.4 us -> 16.9 us  [local(): every = lax.all_to_all(values, peers_order, 0, 0, tiled=True)]
    pallas_call x1, Pallas kernels: 4.22 us -> 1.63 us  [local(): pl.pallas_call(functools.partial(attend, scale, page_len, sender_of(seq,...]
    all_to_all x1, waiting for transfers between devices: 10.5 us -> 12.5 us  [local(): recv = lax.all_to_all(sent, peers_order, 0, 0, tiled=True)]
    all_to_all x1, blocking collectives: 33 us -> 34.5 us  [local(): peers = lax.all_to_all(partial, peers_order, 0, 0, tiled=True)]
  transfers between devices with their start and end apart: 2 -> 2, of which waited for: 2 -> 2; matrix products, arithmetic and copies ran while one was open for 0% -> 0% of each run, Pallas kernels for 8% -> 7%
where the time goes in v5:
time: 103 us; the launch traced here: 102 us
  blocking collectives  51.4 us (50%)
  starting transfers between devices  23.9 us (23%)
  waiting for transfers between devices  13.4 us (13%)
  Pallas kernels  12.1 us (12%)
    all_to_all x1, blocking collectives, local(): peers = lax.all_to_all(partial, peers_order, 0, 0, tiled=True)  34.5 us
    all_to_all x1, starting transfers between devices, local(): recv = lax.all_to_all(sent, peers_order, 0, 0, tiled=True)  21 us
    all_to_all x1, blocking collectives, local(): every = lax.all_to_all(values, peers_order, 0, 0, tiled=True)  16.9 us
    all_to_all x1, waiting for transfers between devices, local(): recv = lax.all_to_all(sent, peers_order, 0, 0, tiled=True)  12.5 us
    pallas_call x1, Pallas kernels, local(): pl.pallas_call(functools.partial(score_rope, scale, page_len), out_shape=...  4.35 us
    pallas_call x1, Pallas kernels, local(): pl.pallas_call(functools.partial(order_slots, page_len), out_shape=jax.Sh...  3.26 us
    ppermute x1, starting transfers between devices, local(): both = half + lax.ppermute(half, 'mp', [(0, 1), (1, 0)])  2.96 us
    pallas_call x1, Pallas kernels, local(): pl.pallas_call(send_query, in_specs=[pl.BlockSpec(memory_space=pltpu.HBM)...  2.41 us
  transfers between devices with their start and end apart: 2, of which 2 were waited for; matrix products, arithmetic and copies ran while one was open for 0% of the time, Pallas kernels for 7%

profile of v5, /device:TPU:641, one launch (start us, length us, event | category | flops | bytes accessed | tf_op | source)
XLA Modules:
  0.0 102.1 jit_solution(3868255874085685099)
XLA Ops:
  0.0 0.0 copy-start
  0.0 0.0 copy-start.1
  0.0 2.4 %shard_map.92 = bf16[64,40,128]{2,1,0:T(8,128)(2,1)} custom-call(bf16[8,64,128]{2,1,0:T(8,128)(2,1)} %q_hbm.2, bf16[64,8,128]{2,1,0:T(8,128)(2,1)} %bitcast.12, bf16[64,8,128]{2,1,0:T(8,128)(2,1)} %v_hbm.1), custom_call_target="tpu_custom_call" | custom-call | tf_op jit(solution)/shard_map/pallas_call | solution.py:314
  2.4 21.0 %all-to-all-start = ((bf16[64,40,128]{2,1,0:T(8,128)(2,1)}), bf16[64,40,128]{2,1,0:T(8,128)(2,1)S(1)}, u32[]{:S(2)}, u32[]{:S(2)}) async-start(bf16[64,40,128]{2,1,0:T(8,128)(2,1)} %shard_map.92), calls=%async_computation | async-start | bytes 1310720 | tf_op jit(solution)/shard_map/all_to_all | solution.py:326
  23.4 0.0 copy-done.1
  23.4 3.3 %shard_map.91.order_ref = s32[1,256]{1,0:T(1,128)S(1)} custom-call(s32[1]{0:T(128)} %bitcast.first_ref, s32[8]{0:T(128)S(1)} %copy-done.1, s32[8,2048]{1,0:T(8,128)} %table_hbm.1), custom_call_target="tpu_custom_call" | custom-call | tf_op jit(solution)/shard_map/pallas_call | solution.py:334
  26.7 4.4 %shard_map.93.rope_hbm = f32[40,64,256]{2,1,0:T(8,128)} custom-call(s32[1,256]{1,0:T(1,128)S(1)} %shard_map.91.order_ref, bf16[8,64,64]{2,1,0:T(8,128)(2,1)} %q_hbm.3, bf16[16,32,8,128]{3,2,1,0:T(8,128)(2,1)} %bitcast.11), custom_call_target="tpu_custom_call" | custom-call | tf_op jit(solution)/shard_map/pallas_call | solution.py:349
  31.1 12.5 %all-to-all-done.recv_ref = bf16[64,40,128]{2,1,0:T(8,128)(2,1)S(1)} async-done(((bf16[64,40,128]{2,1,0:T(8,128)(2,1)}), bf16[64,40,128]{2,1,0:T(8,128)(2,1)S(1)}, u32[]{:S(2)}, u32[]{:S(2)}) %all-to-all-start) | async-done | bytes 655392 | tf_op jit(solution)/shard_map/all_to_all | solution.py:326
  43.6 1.6 %shard_map.94 = (bf16[64,8,640]{2,1,0:T(8,128)(2,1)S(1)}, bf16[64,8,128]{2,1,0:T(8,128)(2,1)S(1)}) custom-call(s32[1,256]{1,0:T(1,128)S(1)} %shard_map.91.order_ref, bf16[64,40,128]{2,1,0:T(8,128)(2,1)S(1)} %all-to-all-done.recv_ref, f32[40,64,256]{2,1,0:T(8,128)} %shard_map.93.rope_hbm, bf16[128,64,512]{2,1,0:T(8,128)(2,1)} %latent_hbm.1), custom_call_target="tpu_custom_call" | custom-call | tf_op jit(solution)/shard_map/pallas_call | solution.py:365
  45.2 34.5 %all_to_all.15.peers_ref = bf16[64,8,640]{2,1,0:T(8,128)(2,1)S(1)} all-to-all(bf16[64,8,640]{2,1,0:T(8,128)(2,1)S(1)} %get-tuple-element.7), channel_id=1, replica_groups=mesh['groups'=2,'seq_0'=2,'seq_1'=2,'seq_2'=2,'seq_3'=2,'seq_4'=2,'seq_5..., dimensions={0} | all-to-all | bytes 1310720 | tf_op jit(solution)/shard_map/all_to_all | solution.py:390
  79.8 0.4 shard_map.95
  80.2 16.9 %all_to_all.16 = bf16[64,8,128]{2,1,0:T(8,128)(2,1)S(1)} all-to-all(bf16[64,8,128]{2,1,0:T(8,128)(2,1)S(1)} %shard_map.95), channel_id=1, replica_groups=mesh['groups'=2,'seq_0'=2,'seq_1'=2,'seq_2'=2,'seq_3'=2,'seq_4'=2,'seq_5..., dimensions={0} | all-to-all | bytes 262144 | tf_op jit(solution)/shard_map/all_to_all | solution.py:397
  97.1 0.0 copy-done
  97.1 0.6 fusion
  97.7 3.0 %collective-permute-start = (f32[8,112]{1,0:T(8,128)S(1)}, f32[8,112]{1,0:T(8,128)S(1)}, u32[]{:S(2)}, u32[]{:S(2)}) collective-permute-start(f32[8,112]{1,0:T(8,128)S(1)} %fusion), channel_id=1, source_target_pairs={{0,1},{1,0},{2,3},{3,2},{4,5},{5,4},{6,7},{7,6},{8,9},{9,8},{10,11... | collective-permute-start | bytes 10760 | tf_op jit(solution)/shard_map/ppermute | solution.py:400
  100.6 0.8 collective-permute-done
  101.4 0.7 dynamic-slice_convert_fusion
  (1 shorter events, 0.0 us)
Async XLA Ops:
  0.0 97.1 %copy-start = (bf16[8192,112]{0,1:T(8,128)(2,1)S(1)}, bf16[8192,112]{0,1:T(8,128)(2,1)}, u32[]{:S(2)}) copy-start(bf16[8192,112]{0,1:T(8,128)(2,1)} %param.15) | copy-start | bytes 5505028
  0.0 23.4 %copy-start.1 = (s32[8]{0:T(128)S(1)}, s32[8]{0:T(128)}, u32[]{:S(2)}) copy-start(s32[8]{0:T(128)} %lengths_ref.1) | copy-start | bytes 100
  2.4 41.2 %all-to-all-start = ((bf16[64,40,128]{2,1,0:T(8,128)(2,1)}), bf16[64,40,128]{2,1,0:T(8,128)(2,1)S(1)}, u32[]{:S(2)}, u32[]{:S(2)}) async-start(bf16[64,40,128]{2,1,0:T(8,128)(2,1)} %shard_map.92), calls=%async_computation | async-start | bytes 1310720 | tf_op jit(solution)/shard_map/all_to_all | solution.py:326
  97.7 3.8 %collective-permute-start = (f32[8,112]{1,0:T(8,128)S(1)}, f32[8,112]{1,0:T(8,128)S(1)}, u32[]{:S(2)}, u32[]{:S(2)}) collective-permute-start(f32[8,112]{1,0:T(8,128)S(1)} %fusion), channel_id=1, source_target_pairs={{0,1},{1,0},{2,3},{3,2},{4,5},{5,4},{6,7},{7,6},{8,9},{9,8},{10,11... | collective-permute-start | bytes 10760 | tf_op jit(solution)/shard_map/ppermute | solution.py:400

commit v6 on v5

--- a/solution.py
+++ b/solution.py
@@ -11,7 +11,7 @@
 NEG = -1e30
 LANES = 128
 GROUP = 4
-BATCH = 4
+BATCH = 6
 NT = (((1,), (1,)), ((), ()))
 
 
@@ -194,7 +194,7 @@
         batch = pl.ds(step * BATCH, BATCH)
         pltpu.make_async_copy(rope_hbm.at[batch], scores.at[batch], rope_sems.at[step]).start()
 
-    ahead = 3
+    ahead = 2
     for step in range(ahead):
 
         @pl.when(step < steps)

time: 103 us -> 102 us (level); the launches traced: 102 us -> 102 us
  no operation moved by 1% of the time
where the time goes in v6:
time: 102 us
  blocking collectives  51.6 us (51%)
  starting transfers between devices  23.9 us (23%)
  waiting for transfers between devices  13.3 us (13%)
  Pallas kernels  12.1 us (12%)
    all_to_all x1, blocking collectives, local(): peers = lax.all_to_all(partial, peers_order, 0, 0, tiled=True)  34.7 us
    all_to_all x1, starting transfers between devices, local(): recv = lax.all_to_all(sent, peers_order, 0, 0, tiled=True)  21 us
    all_to_all x1, blocking collectives, local(): every = lax.all_to_all(values, peers_order, 0, 0, tiled=True)  16.9 us
    all_to_all x1, waiting for transfers between devices, local(): recv = lax.all_to_all(sent, peers_order, 0, 0, tiled=True)  12.5 us
    pallas_call x1, Pallas kernels, local(): pl.pallas_call(functools.partial(score_rope, scale, page_len), out_shape=...  4.39 us
    pallas_call x1, Pallas kernels, local(): pl.pallas_call(functools.partial(order_slots, page_len), out_shape=jax.Sh...  3.26 us
    ppermute x1, starting transfers between devices, local(): both = half + lax.ppermute(half, 'mp', [(0, 1), (1, 0)])  2.87 us
    pallas_call x1, Pallas kernels, local(): pl.pallas_call(send_query, in_specs=[pl.BlockSpec(memory_space=pltpu.HBM)...  2.4 us
  transfers between devices with their start and end apart: 2, of which 2 were waited for; matrix products, arithmetic and copies ran while one was open for 0% of the time, Pallas kernels for 7%

profile of v6, /device:TPU:641, one launch (start us, length us, event | category | flops | bytes accessed | tf_op | source)
XLA Modules:
  0.0 102.1 jit_solution(13183478732902057266)
XLA Ops:
  0.0 0.0 copy-start
  0.0 0.0 copy-start.1
  0.0 2.4 %shard_map.92 = bf16[64,40,128]{2,1,0:T(8,128)(2,1)} custom-call(bf16[8,64,128]{2,1,0:T(8,128)(2,1)} %q_hbm.2, bf16[64,8,128]{2,1,0:T(8,128)(2,1)} %bitcast.12, bf16[64,8,128]{2,1,0:T(8,128)(2,1)} %v_hbm.1), custom_call_target="tpu_custom_call" | custom-call | tf_op jit(solution)/shard_map/pallas_call | solution.py:314
  2.4 21.0 %all-to-all-start = ((bf16[64,40,128]{2,1,0:T(8,128)(2,1)}), bf16[64,40,128]{2,1,0:T(8,128)(2,1)S(1)}, u32[]{:S(2)}, u32[]{:S(2)}) async-start(bf16[64,40,128]{2,1,0:T(8,128)(2,1)} %shard_map.92), calls=%async_computation | async-start | bytes 1310720 | tf_op jit(solution)/shard_map/all_to_all | solution.py:326
  23.4 0.0 copy-done.1
  23.4 3.3 %shard_map.91.order_ref = s32[1,256]{1,0:T(1,128)S(1)} custom-call(s32[1]{0:T(128)} %bitcast.first_ref, s32[8]{0:T(128)S(1)} %copy-done.1, s32[8,2048]{1,0:T(8,128)} %table_hbm.1), custom_call_target="tpu_custom_call" | custom-call | tf_op jit(solution)/shard_map/pallas_call | solution.py:334
  26.7 4.4 %shard_map.93.rope_hbm = f32[42,64,256]{2,1,0:T(8,128)} custom-call(s32[1,256]{1,0:T(1,128)S(1)} %shard_map.91.order_ref, bf16[8,64,64]{2,1,0:T(8,128)(2,1)} %q_hbm.3, bf16[16,32,8,128]{3,2,1,0:T(8,128)(2,1)} %bitcast.11), custom_call_target="tpu_custom_call" | custom-call | tf_op jit(solution)/shard_map/pallas_call | solution.py:349
  31.1 12.5 %all-to-all-done.recv_ref = bf16[64,40,128]{2,1,0:T(8,128)(2,1)S(1)} async-done(((bf16[64,40,128]{2,1,0:T(8,128)(2,1)}), bf16[64,40,128]{2,1,0:T(8,128)(2,1)S(1)}, u32[]{:S(2)}, u32[]{:S(2)}) %all-to-all-start) | async-done | bytes 655392 | tf_op jit(solution)/shard_map/all_to_all | solution.py:326
  43.6 1.6 %shard_map.94 = (bf16[64,8,640]{2,1,0:T(8,128)(2,1)S(1)}, bf16[64,8,128]{2,1,0:T(8,128)(2,1)S(1)}) custom-call(s32[1,256]{1,0:T(1,128)S(1)} %shard_map.91.order_ref, bf16[64,40,128]{2,1,0:T(8,128)(2,1)S(1)} %all-to-all-done.recv_ref, f32[42,64,256]{2,1,0:T(8,128)} %shard_map.93.rope_hbm, bf16[128,64,512]{2,1,0:T(8,128)(2,1)} %latent_hbm.1), custom_call_target="tpu_custom_call" | custom-call | tf_op jit(solution)/shard_map/pallas_call | solution.py:365
  45.2 34.7 %all_to_all.15.peers_ref = bf16[64,8,640]{2,1,0:T(8,128)(2,1)S(1)} all-to-all(bf16[64,8,640]{2,1,0:T(8,128)(2,1)S(1)} %get-tuple-element.7), channel_id=1, replica_groups=mesh['groups'=2,'seq_0'=2,'seq_1'=2,'seq_2'=2,'seq_3'=2,'seq_4'=2,'seq_5..., dimensions={0} | all-to-all | bytes 1310720 | tf_op jit(solution)/shard_map/all_to_all | solution.py:390
  79.9 0.4 shard_map.95
  80.3 16.9 %all_to_all.16 = bf16[64,8,128]{2,1,0:T(8,128)(2,1)S(1)} all-to-all(bf16[64,8,128]{2,1,0:T(8,128)(2,1)S(1)} %shard_map.95), channel_id=1, replica_groups=mesh['groups'=2,'seq_0'=2,'seq_1'=2,'seq_2'=2,'seq_3'=2,'seq_4'=2,'seq_5..., dimensions={0} | all-to-all | bytes 262144 | tf_op jit(solution)/shard_map/all_to_all | solution.py:397
  97.2 0.0 copy-done
  97.2 0.6 fusion
  97.8 2.9 %collective-permute-start = (f32[8,112]{1,0:T(8,128)S(1)}, f32[8,112]{1,0:T(8,128)S(1)}, u32[]{:S(2)}, u32[]{:S(2)}) collective-permute-start(f32[8,112]{1,0:T(8,128)S(1)} %fusion), channel_id=1, source_target_pairs={{0,1},{1,0},{2,3},{3,2},{4,5},{5,4},{6,7},{7,6},{8,9},{9,8},{10,11... | collective-permute-start | bytes 10760 | tf_op jit(solution)/shard_map/ppermute | solution.py:400
  100.7 0.8 collective-permute-done
  101.5 0.7 dynamic-slice_convert_fusion
  (1 shorter events, 0.0 us)
Async XLA Ops:
  0.0 97.2 %copy-start = (bf16[8192,112]{0,1:T(8,128)(2,1)S(1)}, bf16[8192,112]{0,1:T(8,128)(2,1)}, u32[]{:S(2)}) copy-start(bf16[8192,112]{0,1:T(8,128)(2,1)} %param.15) | copy-start | bytes 5505028
  0.0 23.4 %copy-start.1 = (s32[8]{0:T(128)S(1)}, s32[8]{0:T(128)}, u32[]{:S(2)}) copy-start(s32[8]{0:T(128)} %lengths_ref.1) | copy-start | bytes 100
  2.4 41.2 %all-to-all-start = ((bf16[64,40,128]{2,1,0:T(8,128)(2,1)}), bf16[64,40,128]{2,1,0:T(8,128)(2,1)S(1)}, u32[]{:S(2)}, u32[]{:S(2)}) async-start(bf16[64,40,128]{2,1,0:T(8,128)(2,1)} %shard_map.92), calls=%async_computation | async-start | bytes 1310720 | tf_op jit(solution)/shard_map/all_to_all | solution.py:326
  97.8 3.7 %collective-permute-start = (f32[8,112]{1,0:T(8,128)S(1)}, f32[8,112]{1,0:T(8,128)S(1)}, u32[]{:S(2)}, u32[]{:S(2)}) collective-permute-start(f32[8,112]{1,0:T(8,128)S(1)} %fusion), channel_id=1, source_target_pairs={{0,1},{1,0},{2,3},{3,2},{4,5},{5,4},{6,7},{7,6},{8,9},{9,8},{10,11... | collective-permute-start | bytes 10760 | tf_op jit(solution)/shard_map/ppermute | solution.py:400

commit v7 on v6

--- a/solution.py
+++ b/solution.py
@@ -397,9 +397,12 @@
     every = lax.all_to_all(values, peers_order, 0, 0, tiled=True)
     flat = jnp.swapaxes(every, 0, 1).reshape(seqs, heads * value_dim)
     half = jnp.dot(flat, w_out, preferred_element_type=f32)
-    both = half + lax.ppermute(half, "mp", [(0, 1), (1, 0)])
-    share = half.shape[1] // lax.axis_size("mp")
-    return lax.dynamic_slice_in_dim(both, lax.axis_index("mp") * share, share, 1).astype(bf16)
+    other = lax.ppermute(half, "mp", [(0, 1), (1, 0)])
+    assert lax.axis_size("mp") == 2
+    share = half.shape[1] // 2
+    low = lax.axis_index("mp") == 0
+    mine = jnp.where(low, half[:, :share], half[:, share:])
+    return (mine + jnp.where(low, other[:, :share], other[:, share:])).astype(bf16)
 
 
 def sender_of(seq, peers_order):

time: 102 us -> 102 us (level)
  blocking collectives: 51.6 us -> 48.8 us
  Pallas kernels: 12.1 us -> 14.9 us
    all_to_all x1, blocking collectives: 34.7 us -> 31.9 us  [local(): peers = lax.all_to_all(partial, peers_order, 0, 0, tiled=True)]
    pallas_call x1, Pallas kernels: 1.58 us -> 4.1 us  [local(): pl.pallas_call(functools.partial(attend, scale, page_len, sender_of(seq,...]
  transfers between devices with their start and end apart: 2 -> 2, of which waited for: 2 -> 2; matrix products, arithmetic and copies ran while one was open for 0% -> 0% of each run, Pallas kernels for 7% -> 8%
where the time goes in v7:
time: 102 us
  blocking collectives  48.8 us (48%)
  starting transfers between devices  23.9 us (23%)
  Pallas kernels  14.9 us (15%)
  waiting for transfers between devices  13 us (13%)
    all_to_all x1, blocking collectives, local(): peers = lax.all_to_all(partial, peers_order, 0, 0, tiled=True)  31.9 us
    all_to_all x1, starting transfers between devices, local(): recv = lax.all_to_all(sent, peers_order, 0, 0, tiled=True)  21 us
    all_to_all x1, blocking collectives, local(): every = lax.all_to_all(values, peers_order, 0, 0, tiled=True)  16.9 us
    all_to_all x1, waiting for transfers between devices, local(): recv = lax.all_to_all(sent, peers_order, 0, 0, tiled=True)  12.2 us
    pallas_call x1, Pallas kernels, local(): pl.pallas_call(functools.partial(score_rope, scale, page_len), out_shape=...  4.69 us
    pallas_call x1, Pallas kernels, local(): pl.pallas_call(functools.partial(attend, scale, page_len, sender_of(seq,...  4.1 us
    pallas_call x1, Pallas kernels, local(): pl.pallas_call(functools.partial(order_slots, page_len), out_shape=jax.Sh...  3.26 us
    ppermute x1, starting transfers between devices, local(): other = lax.ppermute(half, 'mp', [(0, 1), (1, 0)])  2.87 us
  transfers between devices with their start and end apart: 2, of which 2 were waited for; matrix products, arithmetic and copies ran while one was open for 0% of the time, Pallas kernels for 8%

profile of v7, /device:TPU:641, one launch (start us, length us, event | category | flops | bytes accessed | tf_op | source)
XLA Modules:
  0.0 101.9 jit_solution(7498743583450547076)
XLA Ops:
  0.0 0.0 copy-start
  0.0 0.0 copy-start.1
  0.0 2.4 %shard_map.92 = bf16[64,40,128]{2,1,0:T(8,128)(2,1)} custom-call(bf16[8,64,128]{2,1,0:T(8,128)(2,1)} %q_hbm.2, bf16[64,8,128]{2,1,0:T(8,128)(2,1)} %bitcast.12, bf16[64,8,128]{2,1,0:T(8,128)(2,1)} %v_hbm.1), custom_call_target="tpu_custom_call" | custom-call | tf_op jit(solution)/shard_map/pallas_call | solution.py:314
  2.4 21.0 %all-to-all-start = ((bf16[64,40,128]{2,1,0:T(8,128)(2,1)}), bf16[64,40,128]{2,1,0:T(8,128)(2,1)S(1)}, u32[]{:S(2)}, u32[]{:S(2)}) async-start(bf16[64,40,128]{2,1,0:T(8,128)(2,1)} %shard_map.92), calls=%async_computation | async-start | bytes 1310720 | tf_op jit(solution)/shard_map/all_to_all | solution.py:326
  23.4 0.0 copy-done.1
  23.4 3.3 %shard_map.91.order_ref = s32[1,256]{1,0:T(1,128)S(1)} custom-call(s32[1]{0:T(128)} %bitcast.first_ref, s32[8]{0:T(128)S(1)} %copy-done.1, s32[8,2048]{1,0:T(8,128)} %table_hbm.1), custom_call_target="tpu_custom_call" | custom-call | tf_op jit(solution)/shard_map/pallas_call | solution.py:334
  26.7 4.7 %shard_map.93.rope_hbm = f32[42,64,256]{2,1,0:T(8,128)} custom-call(s32[1,256]{1,0:T(1,128)S(1)} %shard_map.91.order_ref, bf16[8,64,64]{2,1,0:T(8,128)(2,1)} %q_hbm.3, bf16[16,32,8,128]{3,2,1,0:T(8,128)(2,1)} %bitcast.11), custom_call_target="tpu_custom_call" | custom-call | tf_op jit(solution)/shard_map/pallas_call | solution.py:349
  31.4 12.2 %all-to-all-done.recv_ref = bf16[64,40,128]{2,1,0:T(8,128)(2,1)S(1)} async-done(((bf16[64,40,128]{2,1,0:T(8,128)(2,1)}), bf16[64,40,128]{2,1,0:T(8,128)(2,1)S(1)}, u32[]{:S(2)}, u32[]{:S(2)}) %all-to-all-start) | async-done | bytes 655392 | tf_op jit(solution)/shard_map/all_to_all | solution.py:326
  43.6 4.1 %shard_map.94 = (bf16[64,8,640]{2,1,0:T(8,128)(2,1)S(1)}, bf16[64,8,128]{2,1,0:T(8,128)(2,1)S(1)}) custom-call(s32[1,256]{1,0:T(1,128)S(1)} %shard_map.91.order_ref, bf16[64,40,128]{2,1,0:T(8,128)(2,1)S(1)} %all-to-all-done.recv_ref, f32[42,64,256]{2,1,0:T(8,128)} %shard_map.93.rope_hbm, bf16[128,64,512]{2,1,0:T(8,128)(2,1)} %latent_hbm.1), custom_call_target="tpu_custom_call" | custom-call | tf_op jit(solution)/shard_map/pallas_call | solution.py:365
  47.7 31.9 %all_to_all.15.peers_ref = bf16[64,8,640]{2,1,0:T(8,128)(2,1)S(1)} all-to-all(bf16[64,8,640]{2,1,0:T(8,128)(2,1)S(1)} %get-tuple-element.7), channel_id=1, replica_groups=mesh['groups'=2,'seq_0'=2,'seq_1'=2,'seq_2'=2,'seq_3'=2,'seq_4'=2,'seq_5..., dimensions={0} | all-to-all | bytes 1310720 | tf_op jit(solution)/shard_map/all_to_all | solution.py:390
  79.6 0.4 shard_map.95
  80.1 16.9 %all_to_all.16 = bf16[64,8,128]{2,1,0:T(8,128)(2,1)S(1)} all-to-all(bf16[64,8,128]{2,1,0:T(8,128)(2,1)S(1)} %shard_map.95), channel_id=1, replica_groups=mesh['groups'=2,'seq_0'=2,'seq_1'=2,'seq_2'=2,'seq_3'=2,'seq_4'=2,'seq_5..., dimensions={0} | all-to-all | bytes 262144 | tf_op jit(solution)/shard_map/all_to_all | solution.py:397
  97.0 0.0 copy-done
  97.0 0.6 fusion
  97.5 2.9 %collective-permute-start = (f32[8,112]{1,0:T(8,128)S(1)}, f32[8,112]{1,0:T(8,128)S(1)}, u32[]{:S(2)}, u32[]{:S(2)}) collective-permute-start(f32[8,112]{1,0:T(8,128)S(1)} %fusion), channel_id=1, source_target_pairs={{0,1},{1,0},{2,3},{3,2},{4,5},{5,4},{6,7},{7,6},{8,9},{9,8},{10,11... | collective-permute-start | bytes 10760 | tf_op jit(solution)/shard_map/ppermute | solution.py:400
  100.4 0.8 collective-permute-done
  101.2 0.7 add_convert_fusion
Async XLA Ops:
  0.0 97.0 %copy-start = (bf16[8192,112]{0,1:T(8,128)(2,1)S(1)}, bf16[8192,112]{0,1:T(8,128)(2,1)}, u32[]{:S(2)}) copy-start(bf16[8192,112]{0,1:T(8,128)(2,1)} %param.15) | copy-start | bytes 5505028
  0.0 23.4 %copy-start.1 = (s32[8]{0:T(128)S(1)}, s32[8]{0:T(128)}, u32[]{:S(2)}) copy-start(s32[8]{0:T(128)} %lengths_ref.1) | copy-start | bytes 100
  2.4 41.2 %all-to-all-start = ((bf16[64,40,128]{2,1,0:T(8,128)(2,1)}), bf16[64,40,128]{2,1,0:T(8,128)(2,1)S(1)}, u32[]{:S(2)}, u32[]{:S(2)}) async-start(bf16[64,40,128]{2,1,0:T(8,128)(2,1)} %shard_map.92), calls=%async_computation | async-start | bytes 1310720 | tf_op jit(solution)/shard_map/all_to_all | solution.py:326
  97.5 3.7 %collective-permute-start = (f32[8,112]{1,0:T(8,128)S(1)}, f32[8,112]{1,0:T(8,128)S(1)}, u32[]{:S(2)}, u32[]{:S(2)}) collective-permute-start(f32[8,112]{1,0:T(8,128)S(1)} %fusion), channel_id=1, source_target_pairs={{0,1},{1,0},{2,3},{3,2},{4,5},{5,4},{6,7},{7,6},{8,9},{9,8},{10,11... | collective-permute-start | bytes 10760 | tf_op jit(solution)/shard_map/ppermute | solution.py:400
